TPU v7x, 8 devices: a whole 2x2x1 slice. The times are simulated.
8 devices in a mesh: dp: 2 (over z, y), cp: 4 (over x, core).
Axes of the slice: x: 2, y: 2, z: 1, core: 2. Of those that a mesh axis runs over, the one named last changes fastest.
Arguments:
- queries: bfloat16 [64, 512, 10, 256], P('dp', 'cp'), parts along dimension 0
- key_states: bfloat16 [64, 512, 256], P('dp', 'cp'), parts along dimension 0
- value_states: bfloat16 [64, 512, 256], P('dp', 'cp'), parts along dimension 0
- segment_ids: int32 [64, 512], P('dp', 'cp'), parts along dimension 0
Outputs:
- output 1: bfloat16 [64, 512, 10, 256], P('dp', 'cp'), parts along dimension 0
- output 2: float32 [64, 512, 10], P('dp', 'cp'), parts along dimension 0
There are 2 independent parts. A program takes and returns all parts, laid end to end along the dimension named above; each array names one.
All inputs are finite; a program needn't handle non-finite values.
Results may differ from a plain program's by a relative error of at most 0.00326493.
Values are sent between devices in bfloat16 or wider.
A program may use at most 1 GiB of HBM per device.

v0:
```python
import jax
import jax.numpy as jnp
from jax import lax
from jax.sharding import PartitionSpec as P

NEG_BIG = -1e30


def attend_block(run_state, q_loc, seg_loc, q_pos, k_blk, v_blk, seg_blk, blk_idx):
    run_max, run_sum, run_acc = run_state
    blk_len = k_blk.shape[1]
    score_scale = q_loc.shape[-1] ** -0.5
    scores = jnp.einsum("crie,cle->cril", q_loc, k_blk, preferred_element_type=jnp.float32) * score_scale
    k_pos = blk_idx * blk_len + jnp.arange(blk_len)
    visible = (k_pos[None, :] <= q_pos[:, None])[None] & (seg_loc[:, :, None] == seg_blk[:, None, :])
    visible = visible[:, :, None, :]
    masked = jnp.where(visible, scores, NEG_BIG)
    new_max = jnp.maximum(run_max, jnp.max(masked, axis=-1))
    weights = jnp.where(visible, jnp.exp(masked - new_max[..., None]), 0.0)
    rescale = jnp.exp(run_max - new_max)
    new_sum = rescale * run_sum + jnp.sum(weights, axis=-1)
    new_acc = rescale[..., None] * run_acc + jnp.einsum("cril,cle->crie", weights.astype(jnp.bfloat16), v_blk, preferred_element_type=jnp.float32)
    return new_max, new_sum, new_acc


def solution(mesh):
    cp_size = mesh.shape["cp"]
    shift_pairs = [(sender, (sender + 1) % cp_size) for sender in range(cp_size)]

    def local_attention(q_loc, k_loc, v_loc, seg_loc):
        batch, seq_dev, heads, head = q_loc.shape
        my_idx = lax.axis_index("cp")
        q_pos = my_idx * seq_dev + jnp.arange(seq_dev)
        init_state = (
            jnp.full((batch, seq_dev, heads), NEG_BIG, jnp.float32),
            jnp.zeros((batch, seq_dev, heads), jnp.float32),
            jnp.zeros((batch, seq_dev, heads, head), jnp.float32),
        )
        first_state = attend_block(init_state, q_loc, seg_loc, q_pos, k_loc, v_loc, seg_loc, my_idx)

        def step_body(step_idx, carry):
            k_cur, v_cur, seg_cur, acc_state = carry
            k_cur = lax.ppermute(k_cur, "cp", shift_pairs)
            v_cur = lax.ppermute(v_cur, "cp", shift_pairs)
            seg_cur = lax.ppermute(seg_cur, "cp", shift_pairs)
            acc_state = lax.cond(
                step_idx <= my_idx,
                lambda prev_state: attend_block(prev_state, q_loc, seg_loc, q_pos, k_cur, v_cur, seg_cur, my_idx - step_idx),
                lambda prev_state: prev_state,
                acc_state,
            )
            return k_cur, v_cur, seg_cur, acc_state

        final_carry = lax.fori_loop(1, cp_size, step_body, (k_loc, v_loc, seg_loc, first_state))
        run_max, run_sum, run_acc = final_carry[3]
        attn_out = (run_acc / run_sum[..., None]).astype(jnp.bfloat16)
        return attn_out, run_max + jnp.log(run_sum)

    return jax.shard_map(
        local_attention,
        mesh=mesh,
        in_specs=(P("dp", "cp", None, None), P("dp", "cp", None), P("dp", "cp", None), P("dp", "cp")),
        out_specs=(P("dp", "cp", None, None), P("dp", "cp", None)),
        check_vma=False,
    )
```

profile of v0, /device:TPU:7, one launch (start us, length us, event | category | flops | bytes accessed | tf_op | source)
XLA Modules:
  0.0 434.1 jit_solution(14436436019826043100)
XLA Ops:
  0.6 3.1 copy.50
  3.7 3.2 copy.51
  6.9 0.1 broadcast_compare_fusion.1
  7.0 1.5 compare_and_fusion.1
  8.5 17.3 %fusion.17 = (f32[32,128,10]{1,2,0:T(8,128)S(1)}, f32[32,128,10,128]{1,3,2,0:T(8,128)}) fusion(pred[32,128,128]{1,2,0:T(8,128)(4,1)S(1)} %compare_and_fusion.1, bf16[32,128,10,256]{3,1,2,0:T(8,128)(2,1)} %param.8, bf16[32,128,256]{2,1,0:T(8,128)(2,1)} %copy.50), kind=kOutput, calls=%fused_computation.28 | convolution fusion | flops 2700042240 | bytes 44728320 | tf_op jit(solution)/shard_map/crie,cle->cril/dot_general | solution.py:13
  25.8 10.7 %fusion.19 = f32[32,128,10]{1,2,0:T(8,128)S(1)} fusion(f32[32,128,10,128]{1,3,2,0:T(8,128)} %get-tuple-element.301, f32[32,128,10]{1,2,0:T(8,128)S(1)} %broadcast_maximum_fusion, pred[32,128,128]{1,2,0:T(8,128)(4,1)S(1)} %compare_and_fusion.1), kind=kLoop, calls=%fused_computation.30 | loop fusion | flops 26173440 | bytes 21823488 | tf_op jit(solution)/shard_map/reduce_sum | solution.py:21
  36.5 0.8 exponential_multiply_fusion
  37.3 25.3 %broadcast_add_fusion.1 = f32[32,128,10,256]{3,1,2,0:T(8,128)} fusion(f32[32,128,10]{1,2,0:T(8,128)S(1)} %get-tuple-element.298, f32[32,128,10,128]{1,3,2,0:T(8,128)} %get-tuple-element.301, f32[32,128,10]{1,2,0:T(8,128)S(1)} %broadcast_maximum_fusion, pred[32,128,128]{1,2,0:T(8,128)(4,1)S(1)} %compare_and_fusion.1, bf16[32,128,256]{2,1,0:T(8,128)(2,1)} %copy.51), kind=kOutput, calls=%fused_computation.25 | convolution fusion | flops 2721054720 | bytes 65863680 | tf_op jit(solution)/shard_map/cril,cle->crie/dot_general | solution.py:22
  62.6 346.7 %while.24 = (s32[]{:T(128)}, bf16[32,128,256]{2,1,0:T(8,128)(2,1)}, bf16[32,128,256]{2,1,0:T(8,128)(2,1)}, s32[32,128]{1,0:T(8,128)S(1)}, f32[32,128,10]{1,2,0:T...) while((s32[]{:T(128)}, bf16[32,128,256]{2,1,0:T(8,128)(2,1)}, ...), condition=%wide.region_7.8_spmd.clone, body=%wide.region_2.7_spmd.clone.sunk | while | flops 5458984960 | bytes 202018224 | solution.py:54
  62.8 0.8 collective-permute-start
  63.6 0.0 collective-permute-start.1
  63.6 1.6 collective-permute-start.2
  65.2 44.0 %collective-permute-done.2 = s32[32,128]{1,0:T(8,128)S(1)} collective-permute-done((s32[32,128]{1,0:T(8,128)S(1)}, s32[32,128]{1,0:T(8,128)S(1)}, u32[]{:S(2)}, u32[]{:S(2)}) %collective-permute-start.2) | collective-permute-done | bytes 16416 | tf_op jit(solution)/shard_map/while/body/eval_jaxpr/ppermute | solution.py:45
  109.2 0.0 collective-permute-done
  109.2 65.2 %conditional.3 = ((f32[32,128,10]{1,2,0:T(8,128)S(1)}, f32[32,128,10]{1,2,0:T(8,128)}, f32[32,128,10,256]{3,1,2,0:T(8,128)})) conditional(s32[]{:T(128)} %convert_element_type.25, (f32[32,128,10]{1,2,0:T(8,128)S(1)}, f32[32,128,10]{1,2,0:T(8,128)}, f32[32,128,10,256]{3,1,2,0:T(8,128)}) %tuple.51, (s32[]{:T(128)}, s32[]{:T(128)}, s32[]{:T(128)}, ...), branch_computations={%region_3.3_spmd, %region_4.6_spmd} | conditional | flops 5458984960 | bytes 176753216 | solution.py:46
  109.3 0.1 broadcast_compare_fusion
  109.4 0.7 compare_and_fusion
  110.1 17.3 %fusion.2 = (f32[32,128,10]{1,2,0:T(8,128)S(1)}, f32[32,128,10,128]{1,3,2,0:T(8,128)}) fusion(pred[32,128,128]{1,2,0:T(8,128)(4,1)S(1)} %compare_and_fusion, bf16[32,128,10,256]{3,1,2,0:T(8,128)(2,1)} %get-tuple-element.211, bf16[32,128,256]{2,1,0:T(8,128)(2,1)} %get-tuple-element.212), kind=kOutput, calls=%fused_computation.4 | convolution fusion | flops 2700042240 | bytes 44728320 | tf_op jit(solution)/shard_map/while/body/eval_jaxpr/cond/branch_1_fun/crie,cle->cril/dot_general | solution.py:13
  127.4 10.7 %fusion.4 = f32[32,128,10]{1,2,0:T(8,128)S(1)} fusion(f32[32,128,10,128]{1,3,2,0:T(8,128)} %get-tuple-element.295, f32[32,128,10]{1,2,0:T(8,128)S(1)} %max.2, pred[32,128,128]{1,2,0:T(8,128)(4,1)S(1)} %compare_and_fusion), kind=kLoop, calls=%fused_computation.6 | loop fusion | flops 26173440 | bytes 21823488 | tf_op jit(solution)/shard_map/while/body/eval_jaxpr/cond/branch_1_fun/reduce_sum | solution.py:21
  138.1 1.7 multiply_add_fusion.1
  139.9 34.5 %multiply_add_fusion = f32[32,128,10,256]{3,1,2,0:T(8,128)} fusion(f32[32,128,10,256]{3,1,2,0:T(8,128)} %get-tuple-element.214, f32[32,128,10]{1,2,0:T(8,128)S(1)} %get-tuple-element.293, f32[32,128,10,128]{1,3,2,0:T(8,128)} %get-tuple-element.295, f32[32,128,10]{1,2,0:T(8,128)S(1)} %max.2, pred[32,128,128]{1,2,0:T(8,128)(4,1)S(1)} %compare_and_fusion, ...), kind=kOutput, calls=%fused_computation.1 | convolution fusion | flops 2731540480 | bytes 107806720 | tf_op jit(solution)/shard_map/while/body/eval_jaxpr/cond/branch_1_fun/cril,cle->crie/dot_general | solution.py:22
  174.4 3.1 copy.41
  177.5 1.3 copy.42
  178.8 1.6 collective-permute-start.1
  180.4 2.5 collective-permute-start.2
  182.9 41.5 %collective-permute-done.2 = s32[32,128]{1,0:T(8,128)S(1)} collective-permute-done((s32[32,128]{1,0:T(8,128)S(1)}, s32[32,128]{1,0:T(8,128)S(1)}, u32[]{:S(2)}, u32[]{:S(2)}) %collective-permute-start.2) | collective-permute-done | bytes 16416 | tf_op jit(solution)/shard_map/while/body/eval_jaxpr/ppermute | solution.py:45
  224.5 65.2 %conditional.3 = ((f32[32,128,10]{1,2,0:T(8,128)S(1)}, f32[32,128,10]{1,2,0:T(8,128)}, f32[32,128,10,256]{3,1,2,0:T(8,128)})) conditional(s32[]{:T(128)} %convert_element_type.25, (f32[32,128,10]{1,2,0:T(8,128)S(1)}, f32[32,128,10]{1,2,0:T(8,128)}, f32[32,128,10,256]{3,1,2,0:T(8,128)}) %tuple.51, (s32[]{:T(128)}, s32[]{:T(128)}, s32[]{:T(128)}, ...), branch_computations={%region_3.3_spmd, %region_4.6_spmd} | conditional | flops 5458984960 | bytes 176753216 | solution.py:46
  224.5 0.1 broadcast_compare_fusion
  224.6 0.7 compare_and_fusion
  225.3 17.3 %fusion.2 = (f32[32,128,10]{1,2,0:T(8,128)S(1)}, f32[32,128,10,128]{1,3,2,0:T(8,128)}) fusion(pred[32,128,128]{1,2,0:T(8,128)(4,1)S(1)} %compare_and_fusion, bf16[32,128,10,256]{3,1,2,0:T(8,128)(2,1)} %get-tuple-element.211, bf16[32,128,256]{2,1,0:T(8,128)(2,1)} %get-tuple-element.212), kind=kOutput, calls=%fused_computation.4 | convolution fusion | flops 2700042240 | bytes 44728320 | tf_op jit(solution)/shard_map/while/body/eval_jaxpr/cond/branch_1_fun/crie,cle->cril/dot_general | solution.py:13
  242.7 10.7 %fusion.4 = f32[32,128,10]{1,2,0:T(8,128)S(1)} fusion(f32[32,128,10,128]{1,3,2,0:T(8,128)} %get-tuple-element.295, f32[32,128,10]{1,2,0:T(8,128)S(1)} %max.2, pred[32,128,128]{1,2,0:T(8,128)(4,1)S(1)} %compare_and_fusion), kind=kLoop, calls=%fused_computation.6 | loop fusion | flops 26173440 | bytes 21823488 | tf_op jit(solution)/shard_map/while/body/eval_jaxpr/cond/branch_1_fun/reduce_sum | solution.py:21
  253.4 1.7 multiply_add_fusion.1
  255.1 34.5 %multiply_add_fusion = f32[32,128,10,256]{3,1,2,0:T(8,128)} fusion(f32[32,128,10,256]{3,1,2,0:T(8,128)} %get-tuple-element.214, f32[32,128,10]{1,2,0:T(8,128)S(1)} %get-tuple-element.293, f32[32,128,10,128]{1,3,2,0:T(8,128)} %get-tuple-element.295, f32[32,128,10]{1,2,0:T(8,128)S(1)} %max.2, pred[32,128,128]{1,2,0:T(8,128)(4,1)S(1)} %compare_and_fusion, ...), kind=kOutput, calls=%fused_computation.1 | convolution fusion | flops 2731540480 | bytes 107806720 | tf_op jit(solution)/shard_map/while/body/eval_jaxpr/cond/branch_1_fun/cril,cle->crie/dot_general | solution.py:22
  289.6 3.1 copy.41
  292.7 1.3 copy.42
  294.1 6.6 %collective-permute-start.2 = (s32[32,128]{1,0:T(8,128)S(1)}, s32[32,128]{1,0:T(8,128)S(1)}, u32[]{:S(2)}, u32[]{:S(2)}) collective-permute-start(s32[32,128]{1,0:T(8,128)S(1)} %get-tuple-element.396), channel_id=1, source_target_pairs={{0,1},{1,2},{2,3},{3,0},{4,5},{5,6},{6,7},{7,4}} | collective-permute-start | bytes 49160 | tf_op jit(solution)/shard_map/while/body/eval_jaxpr/ppermute | solution.py:45
  300.7 39.0 %collective-permute-done.2 = s32[32,128]{1,0:T(8,128)S(1)} collective-permute-done((s32[32,128]{1,0:T(8,128)S(1)}, s32[32,128]{1,0:T(8,128)S(1)}, u32[]{:S(2)}, u32[]{:S(2)}) %collective-permute-start.2) | collective-permute-done | bytes 16416 | tf_op jit(solution)/shard_map/while/body/eval_jaxpr/ppermute | solution.py:45
  339.7 65.2 %conditional.3 = ((f32[32,128,10]{1,2,0:T(8,128)S(1)}, f32[32,128,10]{1,2,0:T(8,128)}, f32[32,128,10,256]{3,1,2,0:T(8,128)})) conditional(s32[]{:T(128)} %convert_element_type.25, (f32[32,128,10]{1,2,0:T(8,128)S(1)}, f32[32,128,10]{1,2,0:T(8,128)}, f32[32,128,10,256]{3,1,2,0:T(8,128)}) %tuple.51, (s32[]{:T(128)}, s32[]{:T(128)}, s32[]{:T(128)}, ...), branch_computations={%region_3.3_spmd, %region_4.6_spmd} | conditional | flops 5458984960 | bytes 176753216 | solution.py:46
  339.7 0.1 broadcast_compare_fusion
  339.8 0.7 compare_and_fusion
  340.5 17.3 %fusion.2 = (f32[32,128,10]{1,2,0:T(8,128)S(1)}, f32[32,128,10,128]{1,3,2,0:T(8,128)}) fusion(pred[32,128,128]{1,2,0:T(8,128)(4,1)S(1)} %compare_and_fusion, bf16[32,128,10,256]{3,1,2,0:T(8,128)(2,1)} %get-tuple-element.211, bf16[32,128,256]{2,1,0:T(8,128)(2,1)} %get-tuple-element.212), kind=kOutput, calls=%fused_computation.4 | convolution fusion | flops 2700042240 | bytes 44728320 | tf_op jit(solution)/shard_map/while/body/eval_jaxpr/cond/branch_1_fun/crie,cle->cril/dot_general | solution.py:13
  357.9 10.7 %fusion.4 = f32[32,128,10]{1,2,0:T(8,128)S(1)} fusion(f32[32,128,10,128]{1,3,2,0:T(8,128)} %get-tuple-element.295, f32[32,128,10]{1,2,0:T(8,128)S(1)} %max.2, pred[32,128,128]{1,2,0:T(8,128)(4,1)S(1)} %compare_and_fusion), kind=kLoop, calls=%fused_computation.6 | loop fusion | flops 26173440 | bytes 21823488 | tf_op jit(solution)/shard_map/while/body/eval_jaxpr/cond/branch_1_fun/reduce_sum | solution.py:21
  368.6 1.7 multiply_add_fusion.1
  370.3 34.5 %multiply_add_fusion = f32[32,128,10,256]{3,1,2,0:T(8,128)} fusion(f32[32,128,10,256]{3,1,2,0:T(8,128)} %get-tuple-element.214, f32[32,128,10]{1,2,0:T(8,128)S(1)} %get-tuple-element.293, f32[32,128,10,128]{1,3,2,0:T(8,128)} %get-tuple-element.295, f32[32,128,10]{1,2,0:T(8,128)S(1)} %max.2, pred[32,128,128]{1,2,0:T(8,128)(4,1)S(1)} %compare_and_fusion, ...), kind=kOutput, calls=%fused_computation.1 | convolution fusion | flops 2731540480 | bytes 107806720 | tf_op jit(solution)/shard_map/while/body/eval_jaxpr/cond/branch_1_fun/cril,cle->crie/dot_general | solution.py:22
  404.9 3.1 copy.41
  407.9 1.3 copy.42
  409.3 1.7 copy_add_fusion
  411.0 23.1 %divide_convert_fusion = bf16[32,128,10,256]{3,1,2,0:T(8,128)(2,1)} fusion(f32[32,128,10,256]{3,1,2,0:T(8,128)} %get-tuple-element.236, f32[32,128,10]{1,2,0:T(8,128)} %get-tuple-element.237), kind=kLoop, calls=%fused_computation.24 | loop fusion | flops 20971520 | bytes 63078400 | tf_op jit(solution)/shard_map/convert_element_type | solution.py:56
  (28 shorter events, 0.2 us)
Async XLA Ops:
  37.3 25.3 %copy-start = (s32[32,128]{1,0:T(8,128)S(1)}, s32[32,128]{1,0:T(8,128)}, u32[]{:S(2)}) copy-start(s32[32,128]{1,0:T(8,128)} %param.11) | copy-start | bytes 49156
  62.8 46.5 %collective-permute-start = (bf16[32,128,256]{2,1,0:T(8,128)(2,1)}, bf16[32,128,256]{2,1,0:T(8,128)(2,1)}, u32[]{:S(2)}, u32[]{:S(2)}) collective-permute-start(bf16[32,128,256]{2,1,0:T(8,128)(2,1)} %get-tuple-element.394), channel_id=1, source_target_pairs={{0,1},{1,2},{2,3},{3,0},{4,5},{5,6},{6,7},{7,4}} | collective-permute-start | bytes 6291464 | tf_op jit(solution)/shard_map/while/body/eval_jaxpr/ppermute | solution.py:43
  63.6 45.6 %collective-permute-start.1 = (bf16[32,128,256]{2,1,0:T(8,128)(2,1)}, bf16[32,128,256]{2,1,0:T(8,128)(2,1)S(1)}, u32[]{:S(2)}, u32[]{:S(2)}) collective-permute-start(bf16[32,128,256]{2,1,0:T(8,128)(2,1)} %get-tuple-element.395), channel_id=1, source_target_pairs={{0,1},{1,2},{2,3},{3,0},{4,5},{5,6},{6,7},{7,4}} | collective-permute-start | bytes 6291464 | tf_op jit(solution)/shard_map/while/body/eval_jaxpr/ppermute | solution.py:44
  63.6 45.6 %collective-permute-start.2 = (s32[32,128]{1,0:T(8,128)S(1)}, s32[32,128]{1,0:T(8,128)S(1)}, u32[]{:S(2)}, u32[]{:S(2)}) collective-permute-start(s32[32,128]{1,0:T(8,128)S(1)} %get-tuple-element.396), channel_id=1, source_target_pairs={{0,1},{1,2},{2,3},{3,0},{4,5},{5,6},{6,7},{7,4}} | collective-permute-start | bytes 49160 | tf_op jit(solution)/shard_map/while/body/eval_jaxpr/ppermute | solution.py:45
  178.8 45.6 %collective-permute-start = (bf16[32,128,256]{2,1,0:T(8,128)(2,1)}, bf16[32,128,256]{2,1,0:T(8,128)(2,1)}, u32[]{:S(2)}, u32[]{:S(2)}) collective-permute-start(bf16[32,128,256]{2,1,0:T(8,128)(2,1)} %get-tuple-element.394), channel_id=1, source_target_pairs={{0,1},{1,2},{2,3},{3,0},{4,5},{5,6},{6,7},{7,4}} | collective-permute-start | bytes 6291464 | tf_op jit(solution)/shard_map/while/body/eval_jaxpr/ppermute | solution.py:43
  178.8 45.6 %collective-permute-start.1 = (bf16[32,128,256]{2,1,0:T(8,128)(2,1)}, bf16[32,128,256]{2,1,0:T(8,128)(2,1)S(1)}, u32[]{:S(2)}, u32[]{:S(2)}) collective-permute-start(bf16[32,128,256]{2,1,0:T(8,128)(2,1)} %get-tuple-element.395), channel_id=1, source_target_pairs={{0,1},{1,2},{2,3},{3,0},{4,5},{5,6},{6,7},{7,4}} | collective-permute-start | bytes 6291464 | tf_op jit(solution)/shard_map/while/body/eval_jaxpr/ppermute | solution.py:44
  180.4 44.0 %collective-permute-start.2 = (s32[32,128]{1,0:T(8,128)S(1)}, s32[32,128]{1,0:T(8,128)S(1)}, u32[]{:S(2)}, u32[]{:S(2)}) collective-permute-start(s32[32,128]{1,0:T(8,128)S(1)} %get-tuple-element.396), channel_id=1, source_target_pairs={{0,1},{1,2},{2,3},{3,0},{4,5},{5,6},{6,7},{7,4}} | collective-permute-start | bytes 49160 | tf_op jit(solution)/shard_map/while/body/eval_jaxpr/ppermute | solution.py:45
  294.1 45.6 %collective-permute-start = (bf16[32,128,256]{2,1,0:T(8,128)(2,1)}, bf16[32,128,256]{2,1,0:T(8,128)(2,1)}, u32[]{:S(2)}, u32[]{:S(2)}) collective-permute-start(bf16[32,128,256]{2,1,0:T(8,128)(2,1)} %get-tuple-element.394), channel_id=1, source_target_pairs={{0,1},{1,2},{2,3},{3,0},{4,5},{5,6},{6,7},{7,4}} | collective-permute-start | bytes 6291464 | tf_op jit(solution)/shard_map/while/body/eval_jaxpr/ppermute | solution.py:43
  294.1 45.6 %collective-permute-start.1 = (bf16[32,128,256]{2,1,0:T(8,128)(2,1)}, bf16[32,128,256]{2,1,0:T(8,128)(2,1)S(1)}, u32[]{:S(2)}, u32[]{:S(2)}) collective-permute-start(bf16[32,128,256]{2,1,0:T(8,128)(2,1)} %get-tuple-element.395), channel_id=1, source_target_pairs={{0,1},{1,2},{2,3},{3,0},{4,5},{5,6},{6,7},{7,4}} | collective-permute-start | bytes 6291464 | tf_op jit(solution)/shard_map/while/body/eval_jaxpr/ppermute | solution.py:44
  294.1 45.6 %collective-permute-start.2 = (s32[32,128]{1,0:T(8,128)S(1)}, s32[32,128]{1,0:T(8,128)S(1)}, u32[]{:S(2)}, u32[]{:S(2)}) collective-permute-start(s32[32,128]{1,0:T(8,128)S(1)} %get-tuple-element.396), channel_id=1, source_target_pairs={{0,1},{1,2},{2,3},{3,0},{4,5},{5,6},{6,7},{7,4}} | collective-permute-start | bytes 49160 | tf_op jit(solution)/shard_map/while/body/eval_jaxpr/ppermute | solution.py:45
where the time goes:
time: 435 us; the launch traced here: 434 us
  matrix products  198 us (46%)
  waiting for transfers between devices  125 us (29%)
  other arithmetic  77.7 us (18%)
  local copies, waits for them, and re-layouts  19.6 us (5%)
  starting transfers between devices  13.2 us (3%)
    dot_general x4, matrix products, attend_block(): jnp.einsum('cril,cle->crie', weights.astype(jnp.bfloat16), v_blk, preferr...  129 us
    ppermute x3, waiting for transfers between devices, step_body(): seg_cur = lax.ppermute(seg_cur, 'cp', shift_pairs)  125 us
    dot_general x4, matrix products, attend_block(): jnp.einsum('crie,cle->cril', q_loc, k_blk, preferred_element_type=jnp.flo...  69.2 us
    reduce_sum x4, other arithmetic, attend_block(): new_sum = rescale * run_sum + jnp.sum(weights, axis=-1)  42.8 us
    convert_element_type x1, other arithmetic, local_attention(): attn_out = (run_acc / run_sum[..., None]).astype(jnp.bfloat16)  23.1 us
    while x9, local copies, waits for them, and re-layouts  13.3 us
    ppermute x3, starting transfers between devices, step_body(): seg_cur = lax.ppermute(seg_cur, 'cp', shift_pairs)  10.7 us
  transfers between devices with their start and end apart: 9, of which 3 were waited for; matrix products, arithmetic and copies ran while one was open for 0% of the time, Pallas kernels for 0%

commit v1 on v0

v1 whole, which is shorter than its diff:
```python
import functools

import jax
import jax.numpy as jnp
from jax import lax
from jax.experimental import pallas as pl
from jax.experimental.pallas import tpu as pltpu
from jax.sharding import PartitionSpec as P


CHUNKS = (8, 8, 8, 4, 4)
LOG2E = 1.4426950408889634


def attend_kernel(first, heads, s_ref, q_ref, own_ref, near_ref, fara_ref, farb_ref, *rest):
    if first:
        o_ref, lse_ref, key_scr, val_scr = rest
    else:
        _, lse_in, o_ref, lse_ref, key_scr, val_scr = rest
    base = s_ref[0]
    step = pl.program_id(0)
    piece = own_ref.shape[1] // 2
    head = q_ref.shape[3]
    group = 2
    scale = head ** -0.5
    cut = s_ref[6 + base + step]
    me = s_ref[1]

    if not first:
        @pl.when(step == 0)
        def _():
            lse_ref[...] = lse_in[...]

    blocks = (own_ref, near_ref, fara_ref, farb_ref)

    def run(count):
        keys = count * piece
        for n in range(count):
            key_scr[n * piece:(n + 1) * piece] = blocks[n][0, :piece]
            val_scr[n * piece:(n + 1) * piece] = blocks[n][0, piece:]
        lane = lax.broadcasted_iota(jnp.int32, (piece, keys), 1)
        k_pos = lane + me * piece
        for n in range(1, count):
            k_pos = jnp.where(lane >= n * piece, lane + s_ref[2 + n] - n * piece, k_pos)
        q_pos = lax.broadcasted_iota(jnp.int32, (piece, keys), 0) + me * piece
        low = jnp.where(q_pos >= cut, cut, 0)
        visible = (k_pos <= q_pos) & (k_pos >= low)
        cap = jnp.where(visible, jnp.inf, -jnp.inf)
        cap = jnp.concatenate([cap] * group, axis=0)
        cols = []
        for g in range(heads // group):
            q = q_ref[0, g * group:(g + 1) * group].reshape(group * piece, head)
            s = lax.dot_general(q, key_scr[:keys], (((1,), (1,)), ((), ())), preferred_element_type=jnp.float32)
            s = jnp.minimum(s, cap)
            m = jnp.max(s, axis=1, keepdims=True)
            p = jnp.exp2((s - m) * (scale * LOG2E))
            l = jnp.sum(p, axis=1, keepdims=True)
            o = jnp.dot(p.astype(jnp.bfloat16), val_scr[:keys], preferred_element_type=jnp.float32)
            o = o * (1.0 / l)
            o_ref[0, g * group:(g + 1) * group] = o.astype(jnp.bfloat16).reshape(group, piece, head)
            e = m * scale + jnp.log(l)
            for j in range(group):
                cols.append(e[j * piece:(j + 1) * piece])
        rows = jnp.concatenate(cols, axis=1).T
        lse_ref[:, pl.ds(base + step, 1), :] = rows[:, None, :]

    @pl.when(me < 2)
    def _():
        run(2)

    @pl.when(me >= 2)
    def _():
        run(4)


def attend(base, size, batch, scalars, q, own, near, fara, farb, prev):
    _, heads, piece, head = q.shape
    first = prev is None
    kv = pl.BlockSpec((1, 2 * piece, head), lambda i, s: (i, 0, 0))
    qspec = pl.BlockSpec((1, heads, piece, head), lambda i, s: (base + i, 0, 0, 0))
    lse = pl.BlockSpec((heads, batch, piece), lambda i, s: (0, 0, 0))
    in_specs = [qspec, kv, kv, kv, kv]
    args = [q, own, near, fara, farb]
    aliases = {}
    if not first:
        in_specs += [pl.BlockSpec(memory_space=pl.ANY), lse]
        args += list(prev)
        aliases = {6: 0}
    return pl.pallas_call(
        functools.partial(attend_kernel, first, heads),
        grid_spec=pltpu.PrefetchScalarGridSpec(
            num_scalar_prefetch=1,
            grid=(size,),
            in_specs=in_specs,
            out_specs=[qspec, lse],
            scratch_shapes=[pltpu.VMEM((4 * piece, head), jnp.bfloat16)] * 2,
        ),
        out_shape=[
            jax.ShapeDtypeStruct(q.shape, jnp.bfloat16),
            jax.ShapeDtypeStruct((heads, batch, piece), jnp.float32),
        ],
        input_output_aliases=aliases,
        compiler_params=pltpu.CompilerParams(dimension_semantics=("arbitrary",)),
        cost_estimate=pl.CostEstimate(
            flops=size * heads * piece * 4 * piece * head * 4,
            bytes_accessed=size * heads * piece * head * 4,
            transcendentals=0,
        ),
    )(scalars.at[0].set(base), *args)


def shift(x, pairs):
    return lax.ppermute(x, "cp", pairs)


def solution(mesh):
    def local(q_loc, k_loc, v_loc, seg_loc):
        batch, piece, _, _ = q_loc.shape
        me = lax.axis_index("cp")
        q = jnp.transpose(q_loc, (0, 2, 1, 3))
        kv = jnp.concatenate([k_loc, v_loc], axis=1)
        bounds = [sum(CHUNKS[:n]) for n in range(len(CHUNKS) + 1)]
        owns = [kv[a:b] for a, b in zip(bounds[:-1], bounds[1:])]
        fara = [shift(x, [(0, 2), (1, 3)]) for x in owns]
        near = [shift(x, [(0, 1), (2, 3)]) for x in owns]
        farb = [shift(x, [(2, 3), (3, 2)]) for x in fara]
        cuts = lax.psum(jnp.sum((seg_loc == 0).astype(jnp.int32), axis=1), "cp")
        head_scalars = jnp.stack([
            jnp.int32(0),
            me,
            jnp.int32(0),
            jnp.where(me % 2 == 1, (me - 1) * piece, 1 << 20),
            jnp.where(me >= 2, (me - 2) * piece, 1 << 20),
            jnp.where(me >= 2, (3 - me) * piece, 1 << 20),
        ]).astype(jnp.int32)
        scalars = jnp.concatenate([head_scalars, cuts])
        state = None
        for n, size in enumerate(CHUNKS):
            state = attend(bounds[n], size, batch, scalars, q, owns[n], near[n], fara[n], farb[n], state)
        out, lse = state
        return jnp.transpose(out, (0, 2, 1, 3)), jnp.transpose(lse, (1, 2, 0))

    return jax.shard_map(
        local,
        mesh=mesh,
        in_specs=(P("dp", "cp", None, None), P("dp", "cp", None), P("dp", "cp", None), P("dp", "cp")),
        out_specs=(P("dp", "cp", None, None), P("dp", "cp", None)),
        check_vma=False,
    )
```

time: 435 us -> 174 us (0.40)
  matrix products: 198 us -> 0 us
  other arithmetic: 77.7 us -> 0.11 us
  Pallas kernels: 0 us -> 59.9 us
  waiting for transfers between devices: 125 us -> 70.2 us
  starting transfers between devices: 13.2 us -> 32.3 us
  local copies, waits for them, and re-layouts: 19.6 us -> 5.78 us
    dot_general x8 -> x0, matrix products: 198 us -> none  [the longest x4 129 us: attend_block(): jnp.einsum('cril,cle->crie', weights.astype(jnp.bfloat16), v_blk, preferr...]
    pallas_call x0 -> x5, Pallas kernels: none -> 59.9 us  [attend(): pl.pallas_call(functools.partial(attend_kernel, first, heads), grid_spec=...]
    ppermute x9 -> x15, waiting for transfers between devices: 125 us -> 70.2 us  [shift(): return lax.ppermute(x, 'cp', pairs)]
    reduce_sum x4 -> x1, other arithmetic: 42.8 us -> 0.11 us  [local(): cuts = lax.psum(jnp.sum((seg_loc == 0).astype(jnp.int32), axis=1), 'cp')]
    convert_element_type x1 -> x0, other arithmetic: 23.1 us -> none  [local_attention(): attn_out = (run_acc / run_sum[..., None]).astype(jnp.bfloat16)]
    ppermute x9 -> x15, starting transfers between devices: 13.2 us -> 32.3 us  [shift(): return lax.ppermute(x, 'cp', pairs)]
    while x9 -> x0, local copies, waits for them, and re-layouts: 13.3 us -> none
    add x8 -> x0, other arithmetic: 6.9 us -> none  [the longest x3 5.16 us: attend_block(): new_sum = rescale * run_sum + jnp.sum(weights, axis=-1)]
  transfers between devices with their start and end apart: 9 -> 15, of which waited for: 3 -> 2; matrix products, arithmetic and copies ran while one was open for 0% -> 1% of each run, Pallas kernels for 0% -> 30%
where the time goes in v1:
time: 174 us; the launch traced here: 173 us
  waiting for transfers between devices  70.2 us (40%)
  Pallas kernels  59.9 us (34%)
  starting transfers between devices  32.3 us (19%)
  local copies, waits for them, and re-layouts  5.78 us (3%)
  blocking collectives  3.16 us (2%)
    ppermute x15, waiting for transfers between devices, shift(): return lax.ppermute(x, 'cp', pairs)  70.2 us
    pallas_call x5, Pallas kernels, attend(): pl.pallas_call(functools.partial(attend_kernel, first, heads), grid_spec=...  59.9 us
    ppermute x15, starting transfers between devices, shift(): return lax.ppermute(x, 'cp', pairs)  32.3 us
    unnamed x41, local copies, waits for them, and re-layouts  4.18 us
  transfers between devices with their start and end apart: 15, of which 2 were waited for; matrix products, arithmetic and copies ran while one was open for 1% of the time, Pallas kernels for 30%

profile of v1, /device:TPU:7, one launch (start us, length us, event | category | flops | bytes accessed | tf_op | source)
XLA Modules:
  0.0 172.6 jit_solution(6670406102548843149)
XLA Ops:
  0.6 1.9 %constant_dynamic-update-slice_fusion.1 = bf16[32,256,256]{2,1,0:T(8,128)(2,1)S(1)} fusion(bf16[32,128,256]{2,1,0:T(8,128)(2,1)} %param.15), kind=kLoop, calls=%fused_computation.2 | loop fusion | bytes 4194304
  2.6 0.3 copy-done.5
  2.9 0.2 constant_dynamic-update-slice_fusion
  3.1 0.0 copy-start.12
  3.1 0.3 fusion
  3.4 1.3 collective-permute-start.13
  4.7 1.3 collective-permute-start.10
  6.0 1.3 collective-permute-start.12
  7.3 1.3 collective-permute-start.7
  8.6 0.9 fusion.1
  9.5 1.3 collective-permute-start.4
  10.8 18.6 %collective-permute-done.13.fara_ref = bf16[8,256,256]{2,1,0:T(8,128)(2,1)} collective-permute-done((bf16[8,256,256]{2,1,0:T(8,128)(2,1)S(1)}, bf16[8,256,256]{2,1,0:T(8,128)(2,1)}, u32[]{:S(2)}, u32[]{:S(2)}) %collective-permute-start.13) | collective-permute-done | bytes 1048608 | tf_op jit(solution)/shard_map/ppermute | solution.py:113
  29.5 4.6 %collective-permute-start.14 = (bf16[8,256,256]{2,1,0:T(8,128)(2,1)}, bf16[8,256,256]{2,1,0:T(8,128)(2,1)}, u32[]{:S(2)}, u32[]{:S(2)}) collective-permute-start(bf16[8,256,256]{2,1,0:T(8,128)(2,1)} %collective-permute-done.13.fara_ref), channel_id=1, source_target_pairs={{2,3},{3,2},{6,7},{7,6}} | collective-permute-start | bytes 3145736 | tf_op jit(solution)/shard_map/ppermute | solution.py:113
  34.0 51.5 %collective-permute-done.4.fara_ref = bf16[4,256,256]{2,1,0:T(8,128)(2,1)S(1)} collective-permute-done((bf16[4,256,256]{2,1,0:T(8,128)(2,1)S(1)}, bf16[4,256,256]{2,1,0:T(8,128)(2,1)S(1)}, u32[]{:S(2)}, u32[]{:S(2)}) %collective-permute-start.4) | collective-permute-done | bytes 524320 | tf_op jit(solution)/shard_map/ppermute | solution.py:113
  85.6 1.3 collective-permute-start.9
  86.8 0.0 collective-permute-done.10.fara_ref
  86.9 4.5 %collective-permute-start.11 = (bf16[8,256,256]{2,1,0:T(8,128)(2,1)}, bf16[8,256,256]{2,1,0:T(8,128)(2,1)}, u32[]{:S(2)}, u32[]{:S(2)}) collective-permute-start(bf16[8,256,256]{2,1,0:T(8,128)(2,1)} %collective-permute-done.10.fara_ref), channel_id=1, source_target_pairs={{2,3},{3,2},{6,7},{7,6}} | collective-permute-start | bytes 3145736 | tf_op jit(solution)/shard_map/ppermute | solution.py:113
  91.4 0.0 collective-permute-done.12.near_ref
  91.4 1.3 collective-permute-start.6
  92.7 0.0 collective-permute-done.7.fara_ref
  92.7 4.0 %collective-permute-start.8 = (bf16[8,256,256]{2,1,0:T(8,128)(2,1)}, bf16[8,256,256]{2,1,0:T(8,128)(2,1)}, u32[]{:S(2)}, u32[]{:S(2)}) collective-permute-start(bf16[8,256,256]{2,1,0:T(8,128)(2,1)} %collective-permute-done.7.fara_ref), channel_id=1, source_target_pairs={{2,3},{3,2},{6,7},{7,6}} | collective-permute-start | bytes 3145736 | tf_op jit(solution)/shard_map/ppermute | solution.py:113
  96.8 0.1 convert_reduce_fusion
  96.9 3.2 %psum.7 = s32[32]{0:T(128)S(1)} all-reduce(s32[32]{0:T(128)S(1)} %convert_reduce_fusion), channel_id=1, replica_groups=mesh['dp'=2,'cp'=4] {'cp'}, use_global_device_ids=true, to_apply=%region_1.0 | all-reduce | flops 32 | bytes 256 | tf_op jit(solution)/shard_map/psum | solution.py:127
  100.1 0.1 concatenate.16
  100.3 0.0 collective-permute-done.14.farb_ref
  100.3 1.3 collective-permute-start.1
  101.6 14.1 %shard_map.59 = (bf16[32,10,128,256]{3,2,1,0:T(8,128)(2,1)}, f32[10,32,128]{2,1,0:T(8,128)}) custom-call(s32[38]{0:T(128)} %copy-done.15, bf16[32,10,128,256]{3,2,1,0:T(8,128)(2,1)} %bitcast.7, bf16[8,256,256]{2,1,0:T(8,128)(2,1)} %copy-done.2, bf16[8,256,256]{2,1,0:T(8,128)(2,1)} %copy-done.6, bf16[8,256,256]{2,1,0:T(8,128)(2,1)} %collective-permute-done.13.fara_ref, ...), custom_call_target="tpu_custom_call" | custom-call | flops 5368709120 | bytes 10485760 | tf_op jit(solution)/shard_map/pallas_call | solution.py:89
  115.8 0.0 collective-permute-done.9.near_ref
  115.8 1.3 collective-permute-start.3
  117.1 0.0 collective-permute-done.11.farb_ref
  117.1 3.1 %collective-permute-start.5 = (bf16[4,256,256]{2,1,0:T(8,128)(2,1)}, bf16[4,256,256]{2,1,0:T(8,128)(2,1)S(1)}, u32[]{:S(2)}, u32[]{:S(2)}) collective-permute-start(bf16[4,256,256]{2,1,0:T(8,128)(2,1)} %copy-done.7), channel_id=1, source_target_pairs={{2,3},{3,2},{6,7},{7,6}} | collective-permute-start | bytes 1572872 | tf_op jit(solution)/shard_map/ppermute | solution.py:113
  120.2 14.4 %shard_map.60 = (bf16[32,10,128,256]{3,2,1,0:T(8,128)(2,1)}, f32[10,32,128]{2,1,0:T(8,128)}) custom-call(s32[38]{0:T(128)} %copy-done.17, bf16[32,10,128,256]{3,2,1,0:T(8,128)(2,1)} %bitcast.8, bf16[8,256,256]{2,1,0:T(8,128)(2,1)} %copy-done.1, bf16[8,256,256]{2,1,0:T(8,128)(2,1)} %collective-permute-done.9.near_ref, ...), custom_call_target="tpu_custom_call", output_to_operand_aliasing={{0}: (6, {})} | custom-call | flops 5368709120 | bytes 10485760 | tf_op jit(solution)/shard_map/pallas_call | solution.py:89
  134.6 0.0 collective-permute-done.1.fara_ref
  134.6 1.3 collective-permute-start
  135.9 0.0 collective-permute-done.6.near_ref
  136.0 3.2 %collective-permute-start.2 = (bf16[4,256,256]{2,1,0:T(8,128)(2,1)}, bf16[4,256,256]{2,1,0:T(8,128)(2,1)S(1)}, u32[]{:S(2)}, u32[]{:S(2)}) collective-permute-start(bf16[4,256,256]{2,1,0:T(8,128)(2,1)} %collective-permute-done.1.fara_ref), channel_id=1, source_target_pairs={{2,3},{3,2},{6,7},{7,6}} | collective-permute-start | bytes 1572872 | tf_op jit(solution)/shard_map/ppermute | solution.py:113
  139.2 0.0 collective-permute-done.8.farb_ref
  139.2 14.3 %shard_map.61 = (bf16[32,10,128,256]{3,2,1,0:T(8,128)(2,1)}, f32[10,32,128]{2,1,0:T(8,128)}) custom-call(s32[38]{0:T(128)} %copy-done.16, bf16[32,10,128,256]{3,2,1,0:T(8,128)(2,1)} %bitcast.9, bf16[8,256,256]{2,1,0:T(8,128)(2,1)} %copy-done, bf16[8,256,256]{2,1,0:T(8,128)(2,1)} %collective-permute-done.6.near_ref, ...), custom_call_target="tpu_custom_call", output_to_operand_aliasing={{0}: (6, {})} | custom-call | flops 5368709120 | bytes 10485760 | tf_op jit(solution)/shard_map/pallas_call | solution.py:89
  153.5 0.0 collective-permute-done.3.near_ref
  153.5 0.0 collective-permute-done.5.farb_ref
  153.5 0.8 copy-done.8
  154.3 0.2 copy-done.9
  154.5 8.6 %shard_map.62 = (bf16[32,10,128,256]{3,2,1,0:T(8,128)(2,1)}, f32[10,32,128]{2,1,0:T(8,128)}) custom-call(s32[38]{0:T(128)} %copy-done.14, bf16[32,10,128,256]{3,2,1,0:T(8,128)(2,1)} %bitcast.10, bf16[4,256,256]{2,1,0:T(8,128)(2,1)} %copy-done.4, bf16[4,256,256]{2,1,0:T(8,128)(2,1)} %copy-done.8, ...), custom_call_target="tpu_custom_call", output_to_operand_aliasing={{0}: (6, {})} | custom-call | flops 2684354560 | bytes 5242880 | tf_op jit(solution)/shard_map/pallas_call | solution.py:89
  163.0 0.0 collective-permute-done.near_ref
  163.1 0.0 collective-permute-done.2.farb_ref
  163.1 0.8 copy-done.10
  163.8 0.2 copy-done.11
  164.0 8.6 %shard_map.63 = (bf16[32,10,128,256]{3,2,1,0:T(8,128)(2,1)}, f32[10,32,128]{2,1,0:T(8,128)}) custom-call(s32[38]{0:T(128)} %copy-done.13, bf16[32,10,128,256]{3,2,1,0:T(8,128)(2,1)} %bitcast.11, bf16[4,256,256]{2,1,0:T(8,128)(2,1)} %get-tuple-element.86.own_ref, bf16[4,256,256]{2,1,0:T(8,128)(2,1)} %copy-done.10, ...), custom_call_target="tpu_custom_call", output_to_operand_aliasing={{0}: (6, {})} | custom-call | flops 2684354560 | bytes 5242880 | tf_op jit(solution)/shard_map/pallas_call | solution.py:89
  (39 shorter events, 0.1 us)
Async XLA Ops:
  0.6 2.2 %copy-start.5 = (bf16[32,128,256]{2,1,0:T(8,128)(2,1)S(1)}, bf16[32,128,256]{2,1,0:T(8,128)(2,1)}, u32[]{:S(2)}) copy-start(bf16[32,128,256]{2,1,0:T(8,128)(2,1)} %param.16) | copy-start | bytes 6291460
  3.1 93.7 %copy-start.12 = (s32[32,128]{1,0:T(8,128)S(1)}, s32[32,128]{1,0:T(8,128)}, u32[]{:S(2)}) copy-start(s32[32,128]{1,0:T(8,128)} %param.17) | copy-start | bytes 49156
  3.4 98.2 %copy-start.2 = (bf16[8,256,256]{2,1,0:T(8,128)(2,1)}, bf16[8,256,256]{2,1,0:T(8,128)(2,1)S(1)}, u32[]{:S(2)}) copy-start(bf16[8,256,256]{2,1,0:T(8,128)(2,1)S(1)} %get-tuple-element.82.own_ref) | copy-start | bytes 3145732
  3.4 112.3 %copy-start = (bf16[8,256,256]{2,1,0:T(8,128)(2,1)}, bf16[8,256,256]{2,1,0:T(8,128)(2,1)S(1)}, u32[]{:S(2)}) copy-start(bf16[8,256,256]{2,1,0:T(8,128)(2,1)S(1)} %get-tuple-element.84.own_ref) | copy-start | bytes 3145732
  3.4 112.3 %copy-start.1 = (bf16[8,256,256]{2,1,0:T(8,128)(2,1)}, bf16[8,256,256]{2,1,0:T(8,128)(2,1)S(1)}, u32[]{:S(2)}) copy-start(bf16[8,256,256]{2,1,0:T(8,128)(2,1)S(1)} %get-tuple-element.83.own_ref) | copy-start | bytes 3145732
  3.4 26.0 %collective-permute-start.13 = (bf16[8,256,256]{2,1,0:T(8,128)(2,1)S(1)}, bf16[8,256,256]{2,1,0:T(8,128)(2,1)}, u32[]{:S(2)}, u32[]{:S(2)}) collective-permute-start(bf16[8,256,256]{2,1,0:T(8,128)(2,1)S(1)} %get-tuple-element.82.own_ref), channel_id=1, source_target_pairs={{0,2},{1,3},{4,6},{5,7}} | collective-permute-start | bytes 3145736 | tf_op jit(solution)/shard_map/ppermute | solution.py:113
  4.7 82.1 %collective-permute-start.10 = (bf16[8,256,256]{2,1,0:T(8,128)(2,1)S(1)}, bf16[8,256,256]{2,1,0:T(8,128)(2,1)}, u32[]{:S(2)}, u32[]{:S(2)}) collective-permute-start(bf16[8,256,256]{2,1,0:T(8,128)(2,1)S(1)} %get-tuple-element.83.own_ref), channel_id=1, source_target_pairs={{0,2},{1,3},{4,6},{5,7}} | collective-permute-start | bytes 3145736 | tf_op jit(solution)/shard_map/ppermute | solution.py:113
  6.0 85.3 %collective-permute-start.12 = (bf16[8,256,256]{2,1,0:T(8,128)(2,1)S(1)}, bf16[8,256,256]{2,1,0:T(8,128)(2,1)S(1)}, u32[]{:S(2)}, u32[]{:S(2)}) collective-permute-start(bf16[8,256,256]{2,1,0:T(8,128)(2,1)S(1)} %get-tuple-element.82.own_ref), channel_id=1, source_target_pairs={{0,1},{2,3},{4,5},{6,7}} | collective-permute-start | bytes 3145736 | tf_op jit(solution)/shard_map/ppermute | solution.py:113
  7.3 85.3 %collective-permute-start.7 = (bf16[8,256,256]{2,1,0:T(8,128)(2,1)S(1)}, bf16[8,256,256]{2,1,0:T(8,128)(2,1)}, u32[]{:S(2)}, u32[]{:S(2)}) collective-permute-start(bf16[8,256,256]{2,1,0:T(8,128)(2,1)S(1)} %get-tuple-element.84.own_ref), channel_id=1, source_target_pairs={{0,2},{1,3},{4,6},{5,7}} | collective-permute-start | bytes 3145736 | tf_op jit(solution)/shard_map/ppermute | solution.py:113
  9.5 83.1 %copy-start.4 = (bf16[4,256,256]{2,1,0:T(8,128)(2,1)}, bf16[4,256,256]{2,1,0:T(8,128)(2,1)S(1)}, u32[]{:S(2)}) copy-start(bf16[4,256,256]{2,1,0:T(8,128)(2,1)S(1)} %get-tuple-element.85.own_ref) | copy-start | bytes 1572868
  9.5 76.0 %collective-permute-start.4 = (bf16[4,256,256]{2,1,0:T(8,128)(2,1)S(1)}, bf16[4,256,256]{2,1,0:T(8,128)(2,1)S(1)}, u32[]{:S(2)}, u32[]{:S(2)}) collective-permute-start(bf16[4,256,256]{2,1,0:T(8,128)(2,1)S(1)} %get-tuple-element.85.own_ref), channel_id=1, source_target_pairs={{0,2},{1,3},{4,6},{5,7}} | collective-permute-start | bytes 1572872 | tf_op jit(solution)/shard_map/ppermute | solution.py:113
  29.5 70.8 %collective-permute-start.14 = (bf16[8,256,256]{2,1,0:T(8,128)(2,1)}, bf16[8,256,256]{2,1,0:T(8,128)(2,1)}, u32[]{:S(2)}, u32[]{:S(2)}) collective-permute-start(bf16[8,256,256]{2,1,0:T(8,128)(2,1)} %collective-permute-done.13.fara_ref), channel_id=1, source_target_pairs={{2,3},{3,2},{6,7},{7,6}} | collective-permute-start | bytes 3145736 | tf_op jit(solution)/shard_map/ppermute | solution.py:113
  85.5 7.2 %copy-start.7 = (bf16[4,256,256]{2,1,0:T(8,128)(2,1)}, bf16[4,256,256]{2,1,0:T(8,128)(2,1)S(1)}, u32[]{:S(2)}) copy-start(bf16[4,256,256]{2,1,0:T(8,128)(2,1)S(1)} %collective-permute-done.4.fara_ref) | copy-start | bytes 1572868
  85.6 30.2 %collective-permute-start.9 = (bf16[8,256,256]{2,1,0:T(8,128)(2,1)S(1)}, bf16[8,256,256]{2,1,0:T(8,128)(2,1)}, u32[]{:S(2)}, u32[]{:S(2)}) collective-permute-start(bf16[8,256,256]{2,1,0:T(8,128)(2,1)S(1)} %get-tuple-element.83.own_ref), channel_id=1, source_target_pairs={{0,1},{2,3},{4,5},{6,7}} | collective-permute-start | bytes 3145736 | tf_op jit(solution)/shard_map/ppermute | solution.py:113
  86.9 30.3 %collective-permute-start.11 = (bf16[8,256,256]{2,1,0:T(8,128)(2,1)}, bf16[8,256,256]{2,1,0:T(8,128)(2,1)}, u32[]{:S(2)}, u32[]{:S(2)}) collective-permute-start(bf16[8,256,256]{2,1,0:T(8,128)(2,1)} %collective-permute-done.10.fara_ref), channel_id=1, source_target_pairs={{2,3},{3,2},{6,7},{7,6}} | collective-permute-start | bytes 3145736 | tf_op jit(solution)/shard_map/ppermute | solution.py:113
  91.4 5.4 %copy-start.6 = (bf16[8,256,256]{2,1,0:T(8,128)(2,1)}, bf16[8,256,256]{2,1,0:T(8,128)(2,1)S(1)}, u32[]{:S(2)}) copy-start(bf16[8,256,256]{2,1,0:T(8,128)(2,1)S(1)} %collective-permute-done.12.near_ref) | copy-start | bytes 3145732
  91.4 44.6 %collective-permute-start.6 = (bf16[8,256,256]{2,1,0:T(8,128)(2,1)S(1)}, bf16[8,256,256]{2,1,0:T(8,128)(2,1)}, u32[]{:S(2)}, u32[]{:S(2)}) collective-permute-start(bf16[8,256,256]{2,1,0:T(8,128)(2,1)S(1)} %get-tuple-element.84.own_ref), channel_id=1, source_target_pairs={{0,1},{2,3},{4,5},{6,7}} | collective-permute-start | bytes 3145736 | tf_op jit(solution)/shard_map/ppermute | solution.py:113
  92.7 46.5 %collective-permute-start.8 = (bf16[8,256,256]{2,1,0:T(8,128)(2,1)}, bf16[8,256,256]{2,1,0:T(8,128)(2,1)}, u32[]{:S(2)}, u32[]{:S(2)}) collective-permute-start(bf16[8,256,256]{2,1,0:T(8,128)(2,1)} %collective-permute-done.7.fara_ref), channel_id=1, source_target_pairs={{2,3},{3,2},{6,7},{7,6}} | collective-permute-start | bytes 3145736 | tf_op jit(solution)/shard_map/ppermute | solution.py:113
  100.2 1.4 copy-start.15
  100.2 15.5 %copy-start.17 = (s32[38]{0:T(128)}, s32[38]{0:T(128)S(1)}, u32[]{:S(2)}) copy-start(s32[38]{0:T(128)S(1)} %constant_dynamic-update-slice_fusion.2.s_ref) | copy-start | bytes 460
  100.2 15.5 %copy-start.16 = (s32[38]{0:T(128)}, s32[38]{0:T(128)S(1)}, u32[]{:S(2)}) copy-start(s32[38]{0:T(128)S(1)} %constant_dynamic-update-slice_fusion.3.s_ref) | copy-start | bytes 460
  100.3 15.5 %copy-start.14 = (s32[38]{0:T(128)}, s32[38]{0:T(128)S(1)}, u32[]{:S(2)}) copy-start(s32[38]{0:T(128)S(1)} %constant_dynamic-update-slice_fusion.4.s_ref) | copy-start | bytes 460
  100.3 15.5 %copy-start.13 = (s32[38]{0:T(128)}, s32[38]{0:T(128)S(1)}, u32[]{:S(2)}) copy-start(s32[38]{0:T(128)S(1)} %constant_dynamic-update-slice_fusion.5.s_ref) | copy-start | bytes 460
  100.3 34.3 %collective-permute-start.1 = (bf16[4,256,256]{2,1,0:T(8,128)(2,1)}, bf16[4,256,256]{2,1,0:T(8,128)(2,1)}, u32[]{:S(2)}, u32[]{:S(2)}) collective-permute-start(bf16[4,256,256]{2,1,0:T(8,128)(2,1)} %get-tuple-element.86.own_ref), channel_id=1, source_target_pairs={{0,2},{1,3},{4,6},{5,7}} | collective-permute-start | bytes 1572872 | tf_op jit(solution)/shard_map/ppermute | solution.py:113
  115.8 37.7 %collective-permute-start.3 = (bf16[4,256,256]{2,1,0:T(8,128)(2,1)}, bf16[4,256,256]{2,1,0:T(8,128)(2,1)S(1)}, u32[]{:S(2)}, u32[]{:S(2)}) collective-permute-start(bf16[4,256,256]{2,1,0:T(8,128)(2,1)} %copy-done.4), channel_id=1, source_target_pairs={{0,1},{2,3},{4,5},{6,7}} | collective-permute-start | bytes 1572872 | tf_op jit(solution)/shard_map/ppermute | solution.py:113
  117.1 36.4 %collective-permute-start.5 = (bf16[4,256,256]{2,1,0:T(8,128)(2,1)}, bf16[4,256,256]{2,1,0:T(8,128)(2,1)S(1)}, u32[]{:S(2)}, u32[]{:S(2)}) collective-permute-start(bf16[4,256,256]{2,1,0:T(8,128)(2,1)} %copy-done.7), channel_id=1, source_target_pairs={{2,3},{3,2},{6,7},{7,6}} | collective-permute-start | bytes 1572872 | tf_op jit(solution)/shard_map/ppermute | solution.py:113
  120.2 14.4 %copy-start.3 = (bf16[4,256,256]{2,1,0:T(8,128)(2,1)S(1)}, bf16[4,256,256]{2,1,0:T(8,128)(2,1)}, u32[]{:S(2)}) copy-start(bf16[4,256,256]{2,1,0:T(8,128)(2,1)} %get-tuple-element.86.own_ref) | copy-start | bytes 1572868
  134.6 28.4 %collective-permute-start = (bf16[4,256,256]{2,1,0:T(8,128)(2,1)S(1)}, bf16[4,256,256]{2,1,0:T(8,128)(2,1)S(1)}, u32[]{:S(2)}, u32[]{:S(2)}) collective-permute-start(bf16[4,256,256]{2,1,0:T(8,128)(2,1)S(1)} %copy-done.3), channel_id=1, source_target_pairs={{0,1},{2,3},{4,5},{6,7}} | collective-permute-start | bytes 1572872 | tf_op jit(solution)/shard_map/ppermute | solution.py:113
  136.0 27.1 %collective-permute-start.2 = (bf16[4,256,256]{2,1,0:T(8,128)(2,1)}, bf16[4,256,256]{2,1,0:T(8,128)(2,1)S(1)}, u32[]{:S(2)}, u32[]{:S(2)}) collective-permute-start(bf16[4,256,256]{2,1,0:T(8,128)(2,1)} %collective-permute-done.1.fara_ref), channel_id=1, source_target_pairs={{2,3},{3,2},{6,7},{7,6}} | collective-permute-start | bytes 1572872 | tf_op jit(solution)/shard_map/ppermute | solution.py:113
  153.5 0.8 copy-start.8
  153.5 1.0 copy-start.9
  163.1 0.8 copy-start.10
  163.1 1.0 copy-start.11

commit v2 on v1

v2 whole, which is shorter than its diff:
```python
import functools

import jax
import jax.numpy as jnp
from jax import lax
from jax.experimental import pallas as pl
from jax.experimental.pallas import tpu as pltpu
from jax.sharding import PartitionSpec as P


CHUNKS = (2, 5, 6, 6, 6, 4, 2, 1)
GROUP = 2
LOG2E = 1.4426950408889634


def attend_kernel(first, base, s_ref, q_ref, kv_ref, near_k_ref, near_v_ref, fara_ref, farb_ref, *rest):
    if first:
        o_ref, lse_ref, vt_scr = rest
    else:
        _, lse_in, o_ref, lse_ref, vt_scr = rest
    step = pl.program_id(0)
    heads, piece, head = q_ref.shape[1:]
    width = GROUP * piece
    scale = head ** -0.5
    cut = s_ref[5 + base + step]
    me = s_ref[0]

    if not first:
        @pl.when(step == 0)
        def _():
            lse_ref[...] = lse_in[...]

    def run(count):
        keys = [kv_ref[0, :piece], near_k_ref[0], fara_ref[0, :piece], farb_ref[0, :piece]][:count]
        vals = [kv_ref[0, piece:], near_v_ref[0], fara_ref[0, piece:], farb_ref[0, piece:]][:count]
        caps = []
        for n in range(count):
            k_pos = lax.broadcasted_iota(jnp.int32, (piece, piece), 0) + s_ref[1 + n]
            q_pos = lax.broadcasted_iota(jnp.int32, (piece, piece), 1) + me * piece
            low = jnp.where(q_pos >= cut, cut, 0)
            caps.append(jnp.where((k_pos <= q_pos) & (k_pos >= low), jnp.inf, -jnp.inf))
            vt_scr[:, n * piece:(n + 1) * piece] = vals[n].T
        cap = jnp.concatenate(caps, axis=0)
        cap = jnp.concatenate([cap] * GROUP, axis=1)
        key = jnp.concatenate(keys, axis=0)
        for g in range(heads // GROUP):
            q = q_ref[0, g * GROUP:(g + 1) * GROUP].reshape(width, head)
            s = lax.dot_general(key, q, (((1,), (1,)), ((), ())), preferred_element_type=jnp.float32)
            s = jnp.minimum(s, cap)
            m = jnp.max(s, axis=0, keepdims=True)
            p = jnp.exp2((s - m) * (scale * LOG2E))
            l = jnp.sum(p, axis=0, keepdims=True)
            o = jnp.dot(vt_scr[:, :count * piece], p.astype(jnp.bfloat16), preferred_element_type=jnp.float32)
            o = o * (1.0 / l)
            o_ref[0, g * GROUP:(g + 1) * GROUP] = o.astype(jnp.bfloat16).T.reshape(GROUP, piece, head)
            e = m * scale + jnp.log(l)
            for j in range(GROUP):
                lse_ref[g * GROUP + j, pl.ds(base + step, 1), :] = e[:, j * piece:(j + 1) * piece]

    @pl.when(me < 2)
    def _():
        run(2)

    @pl.when(me >= 2)
    def _():
        run(4)


def attend(base, size, scalars, q, own, near, fara, farb, prev):
    batch, heads, piece, head = q.shape
    first = prev is None
    kv = pl.BlockSpec((1, 2 * piece, head), lambda i, s: (i, 0, 0))
    half = pl.BlockSpec((1, piece, head), lambda i, s: (base + i, 0, 0))
    qspec = pl.BlockSpec((1, heads, piece, head), lambda i, s: (base + i, 0, 0, 0))
    lse = pl.BlockSpec((heads, batch, piece), lambda i, s: (0, 0, 0))
    in_specs = [qspec, kv, half, half, kv, kv]
    args = [q, own, *near, fara, farb]
    aliases = {}
    if not first:
        in_specs += [pl.BlockSpec(memory_space=pl.ANY), lse]
        args += list(prev)
        aliases = {7: 0}
    return pl.pallas_call(
        functools.partial(attend_kernel, first, base),
        grid_spec=pltpu.PrefetchScalarGridSpec(
            num_scalar_prefetch=1,
            grid=(size,),
            in_specs=in_specs,
            out_specs=[qspec, lse],
            scratch_shapes=[pltpu.VMEM((head, 4 * piece), jnp.bfloat16)],
        ),
        out_shape=[
            jax.ShapeDtypeStruct(q.shape, jnp.bfloat16),
            jax.ShapeDtypeStruct((heads, batch, piece), jnp.float32),
        ],
        input_output_aliases=aliases,
        compiler_params=pltpu.CompilerParams(dimension_semantics=("arbitrary",)),
        cost_estimate=pl.CostEstimate(
            flops=size * heads * piece * 4 * piece * head * 4,
            bytes_accessed=size * heads * piece * head * 4,
            transcendentals=0,
        ),
    )(scalars, *args)


def shift(x, pairs):
    return lax.ppermute(x, "cp", pairs)


ACROSS = [(0, 2), (1, 3)]
BESIDE = [(0, 1), (2, 3)]
SWAP = [(2, 3), (3, 2)]


def solution(mesh):
    def local(q_loc, k_loc, v_loc, seg_loc):
        _, piece, _, _ = q_loc.shape
        me = lax.axis_index("cp")
        q = jnp.transpose(q_loc, (0, 2, 1, 3))
        bounds = [sum(CHUNKS[:n]) for n in range(len(CHUNKS) + 1)]
        owns = [jnp.concatenate([k_loc[a:b], v_loc[a:b]], axis=1) for a, b in zip(bounds[:-1], bounds[1:])]
        seg_a = shift(seg_loc, ACROSS)
        fara = [shift(x, ACROSS) for x in owns]
        seg_n = shift(seg_loc, BESIDE)
        near = [shift(k_loc, BESIDE), shift(v_loc, BESIDE)]
        seg_b = shift(seg_a, SWAP)
        farb = [shift(x, SWAP) for x in fara]

        def zeros(seg, there):
            return jnp.where(there, jnp.sum((seg == 0).astype(jnp.int32), axis=1), 0)

        odd, upper = me % 2 == 1, me >= 2
        cuts = zeros(seg_loc, True) + zeros(seg_n, odd) + zeros(seg_a, upper) + zeros(seg_b, upper)
        head_scalars = jnp.stack([
            me,
            me * piece,
            jnp.where(odd, (me - 1) * piece, 1 << 20),
            jnp.where(upper, (me - 2) * piece, 1 << 20),
            jnp.where(upper, (3 - me) * piece, 1 << 20),
        ]).astype(jnp.int32)
        scalars = jnp.concatenate([head_scalars, cuts])
        state = None
        for n, size in enumerate(CHUNKS):
            state = attend(bounds[n], size, scalars, q, owns[n], near, fara[n], farb[n], state)
        out, lse = state
        return jnp.transpose(out, (0, 2, 1, 3)), jnp.transpose(lse, (1, 2, 0))

    return jax.shard_map(
        local,
        mesh=mesh,
        in_specs=(P("dp", "cp", None, None), P("dp", "cp", None), P("dp", "cp", None), P("dp", "cp")),
        out_specs=(P("dp", "cp", None, None), P("dp", "cp", None)),
        check_vma=False,
    )
```

time: 174 us -> 186 us (1.069)
  waiting for transfers between devices: 70.2 us -> 36.7 us
  Pallas kernels: 59.9 us -> 79.6 us
  starting transfers between devices: 32.3 us -> 43.9 us
  local copies, waits for them, and re-layouts: 5.78 us -> 16.1 us
  other arithmetic: 0.11 us -> 7.25 us
  blocking collectives: 3.16 us -> 0 us
    ppermute x15 -> x21, waiting for transfers between devices: 70.2 us -> 36.7 us  [shift(): return lax.ppermute(x, 'cp', pairs)]
    pallas_call x5 -> x8, Pallas kernels: 59.9 us -> 79.6 us  [attend(): pl.pallas_call(functools.partial(attend_kernel, first, base), grid_spec=p...]
    ppermute x15 -> x21, starting transfers between devices: 32.3 us -> 43.9 us  [shift(): return lax.ppermute(x, 'cp', pairs)]
    slice x2 -> x10, local copies, waits for them, and re-layouts: 1.21 us -> 11.7 us  [the longest x5 7.48 us: local(): k_loc[a:b]]
    concatenate x0 -> x8, other arithmetic: none -> 6.81 us  [local(): jnp.concatenate([k_loc[a:b], v_loc[a:b]], axis=1)]
    psum x1 -> x0, blocking collectives: 3.16 us -> none  [local(): cuts = lax.psum(jnp.sum((seg_loc == 0).astype(jnp.int32), axis=1), 'cp')]
    unnamed x41 -> x48, local copies, waits for them, and re-layouts: 4.18 us -> 3.78 us
  transfers between devices with their start and end apart: 15 -> 21, of which waited for: 2 -> 7; matrix products, arithmetic and copies ran while one was open for 1% -> 11% of each run, Pallas kernels for 30% -> 41%
where the time goes in v2:
time: 186 us; the launch traced here: 185 us
  Pallas kernels  79.6 us (43%)
  starting transfers between devices  43.9 us (24%)
  waiting for transfers between devices  36.7 us (20%)
  local copies, waits for them, and re-layouts  16.1 us (9%)
  other arithmetic  7.25 us (4%)
    pallas_call x8, Pallas kernels, attend(): pl.pallas_call(functools.partial(attend_kernel, first, base), grid_spec=p...  79.6 us
    ppermute x21, starting transfers between devices, shift(): return lax.ppermute(x, 'cp', pairs)  43.9 us
    ppermute x21, waiting for transfers between devices, shift(): return lax.ppermute(x, 'cp', pairs)  36.7 us
    slice x5, local copies, waits for them, and re-layouts, local(): k_loc[a:b]  7.48 us
    concatenate x8, other arithmetic, local(): jnp.concatenate([k_loc[a:b], v_loc[a:b]], axis=1)  6.81 us
    slice x5, local copies, waits for them, and re-layouts, local(): v_loc[a:b]  4.17 us
    unnamed x48, local copies, waits for them, and re-layouts  3.78 us
  transfers between devices with their start and end apart: 21, of which 7 were waited for; matrix products, arithmetic and copies ran while one was open for 11% of the time, Pallas kernels for 41%

profile of v2, /device:TPU:7, one launch (start us, length us, event | category | flops | bytes accessed | tf_op | source)
XLA Modules:
  0.0 184.7 jit_solution(17591057466585452555)
XLA Ops:
  0.6 1.4 collective-permute-start.1
  2.1 1.3 collective-permute-start
  3.4 1.3 collective-permute-start.3
  4.7 1.3 collective-permute-start.4
  6.0 1.6 fusion.3
  7.6 1.6 fusion.4
  9.3 1.3 collective-permute-start.19
  10.6 2.1 %fusion.5 = (bf16[6,128,256]{2,1,0:T(8,128)(2,1)S(1)}, bf16[6,128,256]{2,1,0:T(8,128)(2,1)S(1)}, bf16[6,128,256]{2,1,0:T(8,128)(2,1)}) fusion(bf16[32,128,256]{2,1,0:T(8,128)(2,1)} %param.5), kind=kLoop, calls=%fused_computation.20 | loop fusion | bytes 2359296 | tf_op jit(solution)/shard_map/slice | solution.py:121
  12.6 0.8 slice.48
  13.5 0.8 fusion.6
  14.4 1.3 collective-permute-start.5
  16.4 6.4 %collective-permute-start.20 = (bf16[2,256,256]{2,1,0:T(8,128)(2,1)S(1)}, bf16[2,256,256]{2,1,0:T(8,128)(2,1)S(1)}, u32[]{:S(2)}, u32[]{:S(2)}) collective-permute-start(bf16[2,256,256]{2,1,0:T(8,128)(2,1)S(1)} %collective-permute-done.19.fara_ref), channel_id=1, source_target_pairs={{2,3},{3,2},{6,7},{7,6}} | collective-permute-start | bytes 786440 | tf_op jit(solution)/shard_map/ppermute | solution.py:107
  22.9 1.2 slice.60
  24.2 1.9 %collective-permute-start.2 = (s32[32,128]{1,0:T(8,128)S(1)}, s32[32,128]{1,0:T(8,128)S(1)}, u32[]{:S(2)}, u32[]{:S(2)}) collective-permute-start(s32[32,128]{1,0:T(8,128)S(1)} %collective-permute-done.1), channel_id=1, source_target_pairs={{2,3},{3,2},{6,7},{7,6}} | collective-permute-start | bytes 49160 | tf_op jit(solution)/shard_map/ppermute | solution.py:107
  26.2 1.1 collective-permute-done.2
  27.3 1.3 collective-permute-start.17
  28.6 1.3 collective-permute-start.15
  29.9 0.9 pad_maximum_fusion.1.kv_ref
  31.5 1.3 collective-permute-start.13
  32.8 1.7 slice.52
  34.5 1.7 slice.53
  36.2 1.7 pad_maximum_fusion.5.kv_ref
  37.9 1.9 %pad_maximum_fusion.4.kv_ref = bf16[4,256,256]{2,1,0:T(8,128)(2,1)} fusion(bf16[4,128,256]{2,1,0:T(8,128)(2,1)} %slice.53, bf16[4,128,256]{2,1,0:T(8,128)(2,1)} %slice.52), kind=kLoop, calls=%fused_computation.4 | loop fusion | flops 1048576 | bytes 1048576 | tf_op jit(solution)/shard_map/concatenate | solution.py:121
  39.8 2.1 %pad_maximum_fusion.kv_ref = bf16[6,256,256]{2,1,0:T(8,128)(2,1)} fusion(bf16[6,128,256]{2,1,0:T(8,128)(2,1)} %get-tuple-element.43, bf16[6,128,256]{2,1,0:T(8,128)(2,1)} %get-tuple-element.40), kind=kLoop, calls=%fused_computation | loop fusion | flops 1572864 | bytes 1572864 | tf_op jit(solution)/shard_map/concatenate | solution.py:121
  42.0 3.4 %collective-permute-done.17.fara_ref = bf16[5,256,256]{2,1,0:T(8,128)(2,1)} collective-permute-done((bf16[5,256,256]{2,1,0:T(8,128)(2,1)S(1)}, bf16[5,256,256]{2,1,0:T(8,128)(2,1)}, u32[]{:S(2)}, u32[]{:S(2)}) %collective-permute-start.17) | collective-permute-done | bytes 655392 | tf_op jit(solution)/shard_map/ppermute | solution.py:107
  45.4 1.3 collective-permute-start.11
  46.8 15.4 %collective-permute-done.15.fara_ref = bf16[6,256,256]{2,1,0:T(8,128)(2,1)} collective-permute-done((bf16[6,256,256]{2,1,0:T(8,128)(2,1)S(1)}, bf16[6,256,256]{2,1,0:T(8,128)(2,1)}, u32[]{:S(2)}, u32[]{:S(2)}) %collective-permute-start.15) | collective-permute-done | bytes 786464 | tf_op jit(solution)/shard_map/ppermute | solution.py:107
  62.2 3.5 %collective-permute-start.18 = (bf16[5,256,256]{2,1,0:T(8,128)(2,1)}, bf16[5,256,256]{2,1,0:T(8,128)(2,1)}, u32[]{:S(2)}, u32[]{:S(2)}) collective-permute-start(bf16[5,256,256]{2,1,0:T(8,128)(2,1)} %collective-permute-done.17.fara_ref), channel_id=1, source_target_pairs={{2,3},{3,2},{6,7},{7,6}} | collective-permute-start | bytes 1966088 | tf_op jit(solution)/shard_map/ppermute | solution.py:107
  65.9 13.2 %collective-permute-done.13.fara_ref = bf16[6,256,256]{2,1,0:T(8,128)(2,1)} collective-permute-done((bf16[6,256,256]{2,1,0:T(8,128)(2,1)}, bf16[6,256,256]{2,1,0:T(8,128)(2,1)}, u32[]{:S(2)}, u32[]{:S(2)}) %collective-permute-start.13) | collective-permute-done | bytes 786464 | tf_op jit(solution)/shard_map/ppermute | solution.py:107
  79.1 3.5 %collective-permute-start.16 = (bf16[6,256,256]{2,1,0:T(8,128)(2,1)}, bf16[6,256,256]{2,1,0:T(8,128)(2,1)S(1)}, u32[]{:S(2)}, u32[]{:S(2)}) collective-permute-start(bf16[6,256,256]{2,1,0:T(8,128)(2,1)} %collective-permute-done.15.fara_ref), channel_id=1, source_target_pairs={{2,3},{3,2},{6,7},{7,6}} | collective-permute-start | bytes 2359304 | tf_op jit(solution)/shard_map/ppermute | solution.py:107
  82.9 1.3 collective-permute-start.9
  84.9 1.9 %collective-permute-start.14 = (bf16[6,256,256]{2,1,0:T(8,128)(2,1)}, bf16[6,256,256]{2,1,0:T(8,128)(2,1)}, u32[]{:S(2)}, u32[]{:S(2)}) collective-permute-start(bf16[6,256,256]{2,1,0:T(8,128)(2,1)} %collective-permute-done.13.fara_ref), channel_id=1, source_target_pairs={{2,3},{3,2},{6,7},{7,6}} | collective-permute-start | bytes 2359304 | tf_op jit(solution)/shard_map/ppermute | solution.py:107
  86.8 6.4 %shard_map.59 = (bf16[32,10,128,256]{3,2,1,0:T(8,128)(2,1)}, f32[10,32,128]{2,1,0:T(8,128)}) custom-call(s32[37]{0:T(128)} %concatenate.27.s_ref, bf16[32,10,128,256]{3,2,1,0:T(8,128)(2,1)} %bitcast.8, bf16[2,256,256]{2,1,0:T(8,128)(2,1)} %copy-done.4, bf16[32,128,256]{2,1,0:T(8,128)(2,1)} %copy-done, ...), custom_call_target="tpu_custom_call" | custom-call | flops 1342177280 | bytes 2621440 | tf_op jit(solution)/shard_map/pallas_call | solution.py:83
  93.2 2.7 %collective-permute-done.11.fara_ref = bf16[6,256,256]{2,1,0:T(8,128)(2,1)} collective-permute-done((bf16[6,256,256]{2,1,0:T(8,128)(2,1)}, bf16[6,256,256]{2,1,0:T(8,128)(2,1)}, u32[]{:S(2)}, u32[]{:S(2)}) %collective-permute-start.11) | collective-permute-done | bytes 786464 | tf_op jit(solution)/shard_map/ppermute | solution.py:107
  95.9 1.3 collective-permute-start.7
  97.2 3.5 %collective-permute-start.12 = (bf16[6,256,256]{2,1,0:T(8,128)(2,1)}, bf16[6,256,256]{2,1,0:T(8,128)(2,1)S(1)}, u32[]{:S(2)}, u32[]{:S(2)}) collective-permute-start(bf16[6,256,256]{2,1,0:T(8,128)(2,1)} %collective-permute-done.11.fara_ref), channel_id=1, source_target_pairs={{2,3},{3,2},{6,7},{7,6}} | collective-permute-start | bytes 2359304 | tf_op jit(solution)/shard_map/ppermute | solution.py:107
  100.8 11.8 %shard_map.60 = (bf16[32,10,128,256]{3,2,1,0:T(8,128)(2,1)}, f32[10,32,128]{2,1,0:T(8,128)}) custom-call(s32[37]{0:T(128)} %concatenate.27.s_ref, bf16[32,10,128,256]{3,2,1,0:T(8,128)(2,1)} %bitcast.9, bf16[5,256,256]{2,1,0:T(8,128)(2,1)} %copy-done.2, bf16[32,128,256]{2,1,0:T(8,128)(2,1)} %copy-done, ...), custom_call_target="tpu_custom_call", output_to_operand_aliasing={{0}: (7, {})} | custom-call | flops 3355443200 | bytes 6553600 | tf_op jit(solution)/shard_map/pallas_call | solution.py:83
  112.7 2.9 %collective-permute-start.6 = (bf16[1,256,256]{2,1,0:T(8,128)(2,1)S(1)}, bf16[1,256,256]{2,1,0:T(8,128)(2,1)S(1)}, u32[]{:S(2)}, u32[]{:S(2)}) collective-permute-start(bf16[1,256,256]{2,1,0:T(8,128)(2,1)S(1)} %copy-done.15), channel_id=1, source_target_pairs={{2,3},{3,2},{6,7},{7,6}} | collective-permute-start | bytes 393224 | tf_op jit(solution)/shard_map/ppermute | solution.py:107
  115.6 1.9 %collective-permute-start.8 = (bf16[2,256,256]{2,1,0:T(8,128)(2,1)S(1)}, bf16[2,256,256]{2,1,0:T(8,128)(2,1)S(1)}, u32[]{:S(2)}, u32[]{:S(2)}) collective-permute-start(bf16[2,256,256]{2,1,0:T(8,128)(2,1)S(1)} %collective-permute-done.7.fara_ref), channel_id=1, source_target_pairs={{2,3},{3,2},{6,7},{7,6}} | collective-permute-start | bytes 786440 | tf_op jit(solution)/shard_map/ppermute | solution.py:107
  117.6 2.6 %collective-permute-start.10 = (bf16[4,256,256]{2,1,0:T(8,128)(2,1)}, bf16[4,256,256]{2,1,0:T(8,128)(2,1)S(1)}, u32[]{:S(2)}, u32[]{:S(2)}) collective-permute-start(bf16[4,256,256]{2,1,0:T(8,128)(2,1)} %collective-permute-done.9.fara_ref), channel_id=1, source_target_pairs={{2,3},{3,2},{6,7},{7,6}} | collective-permute-start | bytes 1572872 | tf_op jit(solution)/shard_map/ppermute | solution.py:107
  120.2 13.4 %shard_map.61 = (bf16[32,10,128,256]{3,2,1,0:T(8,128)(2,1)}, f32[10,32,128]{2,1,0:T(8,128)}) custom-call(s32[37]{0:T(128)} %concatenate.27.s_ref, bf16[32,10,128,256]{3,2,1,0:T(8,128)(2,1)} %bitcast.10, bf16[6,256,256]{2,1,0:T(8,128)(2,1)} %copy-done.1, bf16[32,128,256]{2,1,0:T(8,128)(2,1)} %copy-done, ...), custom_call_target="tpu_custom_call", output_to_operand_aliasing={{0}: (7, {})} | custom-call | flops 4026531840 | bytes 7864320 | tf_op jit(solution)/shard_map/pallas_call | solution.py:83
  133.6 13.4 %shard_map.62 = (bf16[32,10,128,256]{3,2,1,0:T(8,128)(2,1)}, f32[10,32,128]{2,1,0:T(8,128)}) custom-call(s32[37]{0:T(128)} %concatenate.27.s_ref, bf16[32,10,128,256]{3,2,1,0:T(8,128)(2,1)} %bitcast.11, bf16[6,256,256]{2,1,0:T(8,128)(2,1)} %pad_maximum_fusion.1.kv_ref, bf16[32,128,256]{2,1,0:T(8,128)(2,1)} %copy-done, ...), custom_call_target="tpu_custom_call", output_to_operand_aliasing={{0}: (7, {})} | custom-call | flops 4026531840 | bytes 7864320 | tf_op jit(solution)/shard_map/pallas_call | solution.py:83
  147.0 0.9 copy-done.7
  147.9 13.4 %shard_map.63 = (bf16[32,10,128,256]{3,2,1,0:T(8,128)(2,1)}, f32[10,32,128]{2,1,0:T(8,128)}) custom-call(s32[37]{0:T(128)} %concatenate.27.s_ref, bf16[32,10,128,256]{3,2,1,0:T(8,128)(2,1)} %bitcast.12, bf16[6,256,256]{2,1,0:T(8,128)(2,1)} %pad_maximum_fusion.kv_ref, bf16[32,128,256]{2,1,0:T(8,128)(2,1)} %copy-done, ...), custom_call_target="tpu_custom_call", output_to_operand_aliasing={{0}: (7, {})} | custom-call | flops 4026531840 | bytes 7864320 | tf_op jit(solution)/shard_map/pallas_call | solution.py:83
  161.3 0.8 copy-done.8
  162.1 9.9 %shard_map.64 = (bf16[32,10,128,256]{3,2,1,0:T(8,128)(2,1)}, f32[10,32,128]{2,1,0:T(8,128)}) custom-call(s32[37]{0:T(128)} %concatenate.27.s_ref, bf16[32,10,128,256]{3,2,1,0:T(8,128)(2,1)} %bitcast.13, bf16[4,256,256]{2,1,0:T(8,128)(2,1)} %pad_maximum_fusion.4.kv_ref, bf16[32,128,256]{2,1,0:T(8,128)(2,1)} %copy-done, ...), custom_call_target="tpu_custom_call", output_to_operand_aliasing={{0}: (7, {})} | custom-call | flops 2684354560 | bytes 5242880 | tf_op jit(solution)/shard_map/pallas_call | solution.py:83
  172.7 6.8 %shard_map.65 = (bf16[32,10,128,256]{3,2,1,0:T(8,128)(2,1)}, f32[10,32,128]{2,1,0:T(8,128)}) custom-call(s32[37]{0:T(128)} %concatenate.27.s_ref, bf16[32,10,128,256]{3,2,1,0:T(8,128)(2,1)} %bitcast.14, bf16[2,256,256]{2,1,0:T(8,128)(2,1)} %pad_maximum_fusion.5.kv_ref, bf16[32,128,256]{2,1,0:T(8,128)(2,1)} %copy-done, ...), custom_call_target="tpu_custom_call", output_to_operand_aliasing={{0}: (7, {})} | custom-call | flops 1342177280 | bytes 2621440 | tf_op jit(solution)/shard_map/pallas_call | solution.py:83
  180.2 4.6 %shard_map.66 = (bf16[32,10,128,256]{3,2,1,0:T(8,128)(2,1)}, f32[10,32,128]{2,1,0:T(8,128)}) custom-call(s32[37]{0:T(128)} %concatenate.27.s_ref, bf16[32,10,128,256]{3,2,1,0:T(8,128)(2,1)} %bitcast.15, bf16[1,256,256]{2,1,0:T(8,128)(2,1)} %copy-done.9, bf16[32,128,256]{2,1,0:T(8,128)(2,1)} %copy-done, ...), custom_call_target="tpu_custom_call", output_to_operand_aliasing={{0}: (7, {})} | custom-call | flops 671088640 | bytes 1310720 | tf_op jit(solution)/shard_map/pallas_call | solution.py:83
  (74 shorter events, 4.2 us)
Async XLA Ops:
  0.6 12.9 %copy-start.3 = (bf16[32,128,256]{2,1,0:T(8,128)(2,1)S(1)}, bf16[32,128,256]{2,1,0:T(8,128)(2,1)}, u32[]{:S(2)}) copy-start(bf16[32,128,256]{2,1,0:T(8,128)(2,1)} %param.6) | copy-start | bytes 6291460
  0.6 13.7 %collective-permute-start.1 = (s32[32,128]{1,0:T(8,128)}, s32[32,128]{1,0:T(8,128)S(1)}, u32[]{:S(2)}, u32[]{:S(2)}) collective-permute-start(s32[32,128]{1,0:T(8,128)} %param.7), channel_id=1, source_target_pairs={{0,2},{1,3},{4,6},{5,7}} | collective-permute-start | bytes 49160 | tf_op jit(solution)/shard_map/ppermute | solution.py:107
  2.1 22.1 %collective-permute-start = (s32[32,128]{1,0:T(8,128)}, s32[32,128]{1,0:T(8,128)S(1)}, u32[]{:S(2)}, u32[]{:S(2)}) collective-permute-start(s32[32,128]{1,0:T(8,128)} %param.7), channel_id=1, source_target_pairs={{0,1},{2,3},{4,5},{6,7}} | collective-permute-start | bytes 49160 | tf_op jit(solution)/shard_map/ppermute | solution.py:107
  3.4 79.5 %collective-permute-start.3 = (bf16[32,128,256]{2,1,0:T(8,128)(2,1)}, bf16[32,128,256]{2,1,0:T(8,128)(2,1)S(1)}, u32[]{:S(2)}, u32[]{:S(2)}) collective-permute-start(bf16[32,128,256]{2,1,0:T(8,128)(2,1)} %param.5), channel_id=1, source_target_pairs={{0,1},{2,3},{4,5},{6,7}} | collective-permute-start | bytes 6291464 | tf_op jit(solution)/shard_map/ppermute | solution.py:107
  4.7 80.2 %collective-permute-start.4 = (bf16[32,128,256]{2,1,0:T(8,128)(2,1)}, bf16[32,128,256]{2,1,0:T(8,128)(2,1)}, u32[]{:S(2)}, u32[]{:S(2)}) collective-permute-start(bf16[32,128,256]{2,1,0:T(8,128)(2,1)} %param.6), channel_id=1, source_target_pairs={{0,1},{2,3},{4,5},{6,7}} | collective-permute-start | bytes 6291464 | tf_op jit(solution)/shard_map/ppermute | solution.py:107
  9.3 5.1 %copy-start.4 = (bf16[2,256,256]{2,1,0:T(8,128)(2,1)}, bf16[2,256,256]{2,1,0:T(8,128)(2,1)S(1)}, u32[]{:S(2)}) copy-start(bf16[2,256,256]{2,1,0:T(8,128)(2,1)S(1)} %pad_maximum_fusion.6.kv_ref) | copy-start | bytes 786436
  9.3 7.1 %collective-permute-start.19 = (bf16[2,256,256]{2,1,0:T(8,128)(2,1)S(1)}, bf16[2,256,256]{2,1,0:T(8,128)(2,1)S(1)}, u32[]{:S(2)}, u32[]{:S(2)}) collective-permute-start(bf16[2,256,256]{2,1,0:T(8,128)(2,1)S(1)} %pad_maximum_fusion.6.kv_ref), channel_id=1, source_target_pairs={{0,2},{1,3},{4,6},{5,7}} | collective-permute-start | bytes 786440 | tf_op jit(solution)/shard_map/ppermute | solution.py:107
  14.4 11.8 %copy-start.9 = (bf16[1,256,256]{2,1,0:T(8,128)(2,1)}, bf16[1,256,256]{2,1,0:T(8,128)(2,1)S(1)}, u32[]{:S(2)}) copy-start(bf16[1,256,256]{2,1,0:T(8,128)(2,1)S(1)} %pad_maximum_fusion.7.kv_ref) | copy-start | bytes 393220
  14.4 11.8 %copy-start.20 = (s32[32,128]{1,0:T(8,128)}, s32[32,128]{1,0:T(8,128)S(1)}, u32[]{:S(2)}) copy-start(s32[32,128]{1,0:T(8,128)S(1)} %collective-permute-done.1) | copy-start | bytes 49156
  14.4 14.2 %collective-permute-start.5 = (bf16[1,256,256]{2,1,0:T(8,128)(2,1)S(1)}, bf16[1,256,256]{2,1,0:T(8,128)(2,1)S(1)}, u32[]{:S(2)}, u32[]{:S(2)}) collective-permute-start(bf16[1,256,256]{2,1,0:T(8,128)(2,1)S(1)} %pad_maximum_fusion.7.kv_ref), channel_id=1, source_target_pairs={{0,2},{1,3},{4,6},{5,7}} | collective-permute-start | bytes 393224 | tf_op jit(solution)/shard_map/ppermute | solution.py:107
  16.4 9.8 %copy-start.10 = (bf16[2,256,256]{2,1,0:T(8,128)(2,1)}, bf16[2,256,256]{2,1,0:T(8,128)(2,1)S(1)}, u32[]{:S(2)}) copy-start(bf16[2,256,256]{2,1,0:T(8,128)(2,1)S(1)} %collective-permute-done.19.fara_ref) | copy-start | bytes 786436
  16.4 14.4 %collective-permute-start.20 = (bf16[2,256,256]{2,1,0:T(8,128)(2,1)S(1)}, bf16[2,256,256]{2,1,0:T(8,128)(2,1)S(1)}, u32[]{:S(2)}, u32[]{:S(2)}) collective-permute-start(bf16[2,256,256]{2,1,0:T(8,128)(2,1)S(1)} %collective-permute-done.19.fara_ref), channel_id=1, source_target_pairs={{2,3},{3,2},{6,7},{7,6}} | collective-permute-start | bytes 786440 | tf_op jit(solution)/shard_map/ppermute | solution.py:107
  22.9 7.9 %copy-start.1 = (bf16[6,256,256]{2,1,0:T(8,128)(2,1)}, bf16[6,256,256]{2,1,0:T(8,128)(2,1)S(1)}, u32[]{:S(2)}) copy-start(bf16[6,256,256]{2,1,0:T(8,128)(2,1)S(1)} %pad_maximum_fusion.2.kv_ref) | copy-start | bytes 2359300
  24.2 8.6 %copy-start.18 = (s32[32,128]{1,0:T(8,128)}, s32[32,128]{1,0:T(8,128)S(1)}, u32[]{:S(2)}) copy-start(s32[32,128]{1,0:T(8,128)S(1)} %collective-permute-done) | copy-start | bytes 49156
  24.2 3.1 %collective-permute-start.2 = (s32[32,128]{1,0:T(8,128)S(1)}, s32[32,128]{1,0:T(8,128)S(1)}, u32[]{:S(2)}, u32[]{:S(2)}) collective-permute-start(s32[32,128]{1,0:T(8,128)S(1)} %collective-permute-done.1), channel_id=1, source_target_pairs={{2,3},{3,2},{6,7},{7,6}} | collective-permute-start | bytes 49160 | tf_op jit(solution)/shard_map/ppermute | solution.py:107
  26.2 13.6 %copy-start.2 = (bf16[5,256,256]{2,1,0:T(8,128)(2,1)}, bf16[5,256,256]{2,1,0:T(8,128)(2,1)S(1)}, u32[]{:S(2)}) copy-start(bf16[5,256,256]{2,1,0:T(8,128)(2,1)S(1)} %pad_maximum_fusion.3.kv_ref) | copy-start | bytes 1966084
  27.3 5.5 %copy-start.22 = (s32[32,128]{1,0:T(8,128)}, s32[32,128]{1,0:T(8,128)S(1)}, u32[]{:S(2)}) copy-start(s32[32,128]{1,0:T(8,128)S(1)} %collective-permute-done.2) | copy-start | bytes 49156
  27.3 18.1 %collective-permute-start.17 = (bf16[5,256,256]{2,1,0:T(8,128)(2,1)S(1)}, bf16[5,256,256]{2,1,0:T(8,128)(2,1)}, u32[]{:S(2)}, u32[]{:S(2)}) collective-permute-start(bf16[5,256,256]{2,1,0:T(8,128)(2,1)S(1)} %pad_maximum_fusion.3.kv_ref), channel_id=1, source_target_pairs={{0,2},{1,3},{4,6},{5,7}} | collective-permute-start | bytes 1966088 | tf_op jit(solution)/shard_map/ppermute | solution.py:107
  28.6 4.3 %copy-start.14 = (bf16[1,256,256]{2,1,0:T(8,128)(2,1)}, bf16[1,256,256]{2,1,0:T(8,128)(2,1)S(1)}, u32[]{:S(2)}) copy-start(bf16[1,256,256]{2,1,0:T(8,128)(2,1)S(1)} %collective-permute-done.5.fara_ref) | copy-start | bytes 393220
  28.6 33.7 %collective-permute-start.15 = (bf16[6,256,256]{2,1,0:T(8,128)(2,1)S(1)}, bf16[6,256,256]{2,1,0:T(8,128)(2,1)}, u32[]{:S(2)}, u32[]{:S(2)}) collective-permute-start(bf16[6,256,256]{2,1,0:T(8,128)(2,1)S(1)} %pad_maximum_fusion.2.kv_ref), channel_id=1, source_target_pairs={{0,2},{1,3},{4,6},{5,7}} | collective-permute-start | bytes 2359304 | tf_op jit(solution)/shard_map/ppermute | solution.py:107
  30.8 0.7 copy-start.11
  31.5 47.6 %collective-permute-start.13 = (bf16[6,256,256]{2,1,0:T(8,128)(2,1)}, bf16[6,256,256]{2,1,0:T(8,128)(2,1)}, u32[]{:S(2)}, u32[]{:S(2)}) collective-permute-start(bf16[6,256,256]{2,1,0:T(8,128)(2,1)} %pad_maximum_fusion.1.kv_ref), channel_id=1, source_target_pairs={{0,2},{1,3},{4,6},{5,7}} | collective-permute-start | bytes 2359304 | tf_op jit(solution)/shard_map/ppermute | solution.py:107
  32.8 13.8 %copy-start.17 = (s32[32,128]{1,0:T(8,128)S(1)}, s32[32,128]{1,0:T(8,128)}, u32[]{:S(2)}) copy-start(s32[32,128]{1,0:T(8,128)} %param.7) | copy-start | bytes 49156
  36.2 29.6 %copy-start.21 = (s32[32,128]{1,0:T(8,128)S(1)}, s32[32,128]{1,0:T(8,128)}, u32[]{:S(2)}) copy-start(s32[32,128]{1,0:T(8,128)} %copy-done.20) | copy-start | bytes 49156
  36.2 46.4 %copy-start.19 = (s32[32,128]{1,0:T(8,128)S(1)}, s32[32,128]{1,0:T(8,128)}, u32[]{:S(2)}) copy-start(s32[32,128]{1,0:T(8,128)} %copy-done.18) | copy-start | bytes 49156
  36.2 46.5 %copy-start.23 = (s32[32,128]{1,0:T(8,128)S(1)}, s32[32,128]{1,0:T(8,128)}, u32[]{:S(2)}) copy-start(s32[32,128]{1,0:T(8,128)} %copy-done.22) | copy-start | bytes 49156
  45.4 50.6 %collective-permute-start.11 = (bf16[6,256,256]{2,1,0:T(8,128)(2,1)}, bf16[6,256,256]{2,1,0:T(8,128)(2,1)}, u32[]{:S(2)}, u32[]{:S(2)}) collective-permute-start(bf16[6,256,256]{2,1,0:T(8,128)(2,1)} %pad_maximum_fusion.kv_ref), channel_id=1, source_target_pairs={{0,2},{1,3},{4,6},{5,7}} | collective-permute-start | bytes 2359304 | tf_op jit(solution)/shard_map/ppermute | solution.py:107
  62.2 35.0 %collective-permute-start.18 = (bf16[5,256,256]{2,1,0:T(8,128)(2,1)}, bf16[5,256,256]{2,1,0:T(8,128)(2,1)}, u32[]{:S(2)}, u32[]{:S(2)}) collective-permute-start(bf16[5,256,256]{2,1,0:T(8,128)(2,1)} %collective-permute-done.17.fara_ref), channel_id=1, source_target_pairs={{2,3},{3,2},{6,7},{7,6}} | collective-permute-start | bytes 1966088 | tf_op jit(solution)/shard_map/ppermute | solution.py:107
  79.1 38.5 %collective-permute-start.16 = (bf16[6,256,256]{2,1,0:T(8,128)(2,1)}, bf16[6,256,256]{2,1,0:T(8,128)(2,1)S(1)}, u32[]{:S(2)}, u32[]{:S(2)}) collective-permute-start(bf16[6,256,256]{2,1,0:T(8,128)(2,1)} %collective-permute-done.15.fara_ref), channel_id=1, source_target_pairs={{2,3},{3,2},{6,7},{7,6}} | collective-permute-start | bytes 2359304 | tf_op jit(solution)/shard_map/ppermute | solution.py:107
  82.9 3.9 %copy-start = (bf16[32,128,256]{2,1,0:T(8,128)(2,1)}, bf16[32,128,256]{2,1,0:T(8,128)(2,1)S(1)}, u32[]{:S(2)}) copy-start(bf16[32,128,256]{2,1,0:T(8,128)(2,1)S(1)} %collective-permute-done.3.near_k_ref) | copy-start | bytes 6291460
  82.9 32.7 %collective-permute-start.9 = (bf16[4,256,256]{2,1,0:T(8,128)(2,1)}, bf16[4,256,256]{2,1,0:T(8,128)(2,1)}, u32[]{:S(2)}, u32[]{:S(2)}) collective-permute-start(bf16[4,256,256]{2,1,0:T(8,128)(2,1)} %pad_maximum_fusion.4.kv_ref), channel_id=1, source_target_pairs={{0,2},{1,3},{4,6},{5,7}} | collective-permute-start | bytes 1572872 | tf_op jit(solution)/shard_map/ppermute | solution.py:107
  84.9 48.7 %collective-permute-start.14 = (bf16[6,256,256]{2,1,0:T(8,128)(2,1)}, bf16[6,256,256]{2,1,0:T(8,128)(2,1)}, u32[]{:S(2)}, u32[]{:S(2)}) collective-permute-start(bf16[6,256,256]{2,1,0:T(8,128)(2,1)} %collective-permute-done.13.fara_ref), channel_id=1, source_target_pairs={{2,3},{3,2},{6,7},{7,6}} | collective-permute-start | bytes 2359304 | tf_op jit(solution)/shard_map/ppermute | solution.py:107
  86.8 9.1 %copy-start.5 = (bf16[2,256,256]{2,1,0:T(8,128)(2,1)S(1)}, bf16[2,256,256]{2,1,0:T(8,128)(2,1)}, u32[]{:S(2)}) copy-start(bf16[2,256,256]{2,1,0:T(8,128)(2,1)} %pad_maximum_fusion.5.kv_ref) | copy-start | bytes 786436
  95.9 16.7 %collective-permute-start.7 = (bf16[2,256,256]{2,1,0:T(8,128)(2,1)S(1)}, bf16[2,256,256]{2,1,0:T(8,128)(2,1)S(1)}, u32[]{:S(2)}, u32[]{:S(2)}) collective-permute-start(bf16[2,256,256]{2,1,0:T(8,128)(2,1)S(1)} %copy-done.5), channel_id=1, source_target_pairs={{0,2},{1,3},{4,6},{5,7}} | collective-permute-start | bytes 786440 | tf_op jit(solution)/shard_map/ppermute | solution.py:107
  97.2 49.8 %collective-permute-start.12 = (bf16[6,256,256]{2,1,0:T(8,128)(2,1)}, bf16[6,256,256]{2,1,0:T(8,128)(2,1)S(1)}, u32[]{:S(2)}, u32[]{:S(2)}) collective-permute-start(bf16[6,256,256]{2,1,0:T(8,128)(2,1)} %collective-permute-done.11.fara_ref), channel_id=1, source_target_pairs={{2,3},{3,2},{6,7},{7,6}} | collective-permute-start | bytes 2359304 | tf_op jit(solution)/shard_map/ppermute | solution.py:107
  100.8 11.9 %copy-start.15 = (bf16[1,256,256]{2,1,0:T(8,128)(2,1)S(1)}, bf16[1,256,256]{2,1,0:T(8,128)(2,1)}, u32[]{:S(2)}) copy-start(bf16[1,256,256]{2,1,0:T(8,128)(2,1)} %copy-done.14) | copy-start | bytes 393220
  112.7 20.9 %copy-start.12 = (bf16[2,256,256]{2,1,0:T(8,128)(2,1)}, bf16[2,256,256]{2,1,0:T(8,128)(2,1)S(1)}, u32[]{:S(2)}) copy-start(bf16[2,256,256]{2,1,0:T(8,128)(2,1)S(1)} %collective-permute-done.7.fara_ref) | copy-start | bytes 786436
  112.7 66.8 %collective-permute-start.6 = (bf16[1,256,256]{2,1,0:T(8,128)(2,1)S(1)}, bf16[1,256,256]{2,1,0:T(8,128)(2,1)S(1)}, u32[]{:S(2)}, u32[]{:S(2)}) collective-permute-start(bf16[1,256,256]{2,1,0:T(8,128)(2,1)S(1)} %copy-done.15), channel_id=1, source_target_pairs={{2,3},{3,2},{6,7},{7,6}} | collective-permute-start | bytes 393224 | tf_op jit(solution)/shard_map/ppermute | solution.py:107
  115.6 56.4 %collective-permute-start.8 = (bf16[2,256,256]{2,1,0:T(8,128)(2,1)S(1)}, bf16[2,256,256]{2,1,0:T(8,128)(2,1)S(1)}, u32[]{:S(2)}, u32[]{:S(2)}) collective-permute-start(bf16[2,256,256]{2,1,0:T(8,128)(2,1)S(1)} %collective-permute-done.7.fara_ref), channel_id=1, source_target_pairs={{2,3},{3,2},{6,7},{7,6}} | collective-permute-start | bytes 786440 | tf_op jit(solution)/shard_map/ppermute | solution.py:107
  117.6 2.6 %copy-start.6 = (bf16[6,256,256]{2,1,0:T(8,128)(2,1)}, bf16[6,256,256]{2,1,0:T(8,128)(2,1)S(1)}, u32[]{:S(2)}) copy-start(bf16[6,256,256]{2,1,0:T(8,128)(2,1)S(1)} %collective-permute-done.16.farb_ref) | copy-start | bytes 2359300
  117.6 43.8 %collective-permute-start.10 = (bf16[4,256,256]{2,1,0:T(8,128)(2,1)}, bf16[4,256,256]{2,1,0:T(8,128)(2,1)S(1)}, u32[]{:S(2)}, u32[]{:S(2)}) collective-permute-start(bf16[4,256,256]{2,1,0:T(8,128)(2,1)} %collective-permute-done.9.fara_ref), channel_id=1, source_target_pairs={{2,3},{3,2},{6,7},{7,6}} | collective-permute-start | bytes 1572872 | tf_op jit(solution)/shard_map/ppermute | solution.py:107
  147.0 0.9 copy-start.7
  161.3 0.8 copy-start.8
  172.0 0.7 copy-start.13
  179.5 0.6 copy-start.16

commit v3 on v2

v3 whole, which is shorter than its diff:
```python
import functools

import jax
import jax.numpy as jnp
from jax import lax
from jax.experimental import pallas as pl
from jax.experimental.pallas import tpu as pltpu
from jax.sharding import PartitionSpec as P


CHUNKS = (4, 8, 8, 7, 5)
BOUNDS = tuple(sum(CHUNKS[:n]) for n in range(len(CHUNKS) + 1))
GROUP = 2
LOG2E = 1.4426950408889634

ACROSS = [(0, 2), (1, 3)]
BESIDE = [(0, 1), (2, 3)]
SWAP = [(2, 3), (3, 2)]


def pack_kernel(ranges, tails, seg_ref, k_ref, v_ref, *rest):
    count = len(ranges)
    outs, (k_scr, v_scr, z_scr, in_sem, out_sem) = rest[:count], rest[count:]
    piece = k_ref.shape[1]
    first = min(a for a, _ in ranges)
    last = max(b for _, b in ranges)
    loads = [
        pltpu.make_async_copy(src.at[pl.ds(first, last - first)], dst.at[pl.ds(first, last - first)], in_sem.at[i])
        for i, (src, dst) in enumerate(((k_ref, k_scr), (v_ref, v_scr)))
    ]
    for load in loads:
        load.start()
    here = jnp.sum((seg_ref[...] == 0).astype(jnp.float32), axis=1, keepdims=True)
    z_scr[...] = jnp.broadcast_to(here, z_scr.shape).astype(jnp.bfloat16)
    for load in loads:
        load.wait()
    for out, (a, b), tail in zip(outs, ranges, tails):
        @pl.loop(0, b - a)
        def _(i):
            for half, src in enumerate((k_scr, v_scr)):
                pltpu.make_async_copy(
                    src.at[a + i], out.at[pl.ds(pl.multiple_of((2 * i + half) * piece, piece), piece)], out_sem
                ).start()

        if tail:
            pltpu.make_async_copy(z_scr, out.at[pl.ds((b - a) * 2 * piece, z_scr.shape[0])], out_sem).start()
    for out in outs:
        pltpu.make_async_copy(out, out, out_sem).wait()


def pack(ranges, tails, seg, k, v):
    batch, piece, head = k.shape
    return pl.pallas_call(
        functools.partial(pack_kernel, ranges, tails),
        in_specs=[pl.BlockSpec(memory_space=pltpu.VMEM)] + [pl.BlockSpec(memory_space=pl.ANY)] * 2,
        out_specs=[pl.BlockSpec(memory_space=pl.ANY)] * len(ranges),
        out_shape=[
            jax.ShapeDtypeStruct(((b - a) * 2 * piece + (batch if tail else 0), head), jnp.bfloat16)
            for (a, b), tail in zip(ranges, tails)
        ],
        scratch_shapes=[
            pltpu.VMEM(k.shape, jnp.bfloat16),
            pltpu.VMEM(k.shape, jnp.bfloat16),
            pltpu.VMEM((batch, head), jnp.bfloat16),
            pltpu.SemaphoreType.DMA((2,)),
            pltpu.SemaphoreType.DMA,
        ],
        cost_estimate=pl.CostEstimate(flops=1 << 20, bytes_accessed=4 * k.size, transcendentals=0),
    )(seg, k, v)


def attend_kernel(first, base, s_ref, q_ref, k_ref, v_ref, near_ref, fara_ref, farb_ref, *rest):
    if first:
        o_ref, lse_ref, k_scr, v_scr = rest
    else:
        _, lse_in, o_ref, lse_ref, k_scr, v_scr = rest
    step = pl.program_id(0)
    seq = base + step
    heads, piece, head = q_ref.shape[1:]
    batch = lse_ref.shape[1]
    width = GROUP * piece
    scale = head ** -0.5
    me, odd = s_ref[0], s_ref[1]
    cut, need = s_ref[2 + seq], s_ref[2 + batch + seq]

    if not first:
        @pl.when(step == 0)
        def _():
            lse_ref[...] = lse_in[...]

    def put(slot, k, v):
        k_scr[slot * piece:(slot + 1) * piece] = k
        v_scr[slot * piece:(slot + 1) * piece] = v

    put(0, k_ref[0], v_ref[0])

    @pl.when(odd == 1)
    def _():
        for slot, ref in enumerate((near_ref, fara_ref, farb_ref)):
            put(slot + 1, ref[:piece], ref[piece:])

    @pl.when(odd == 0)
    def _():
        for slot, ref in enumerate((farb_ref, fara_ref)):
            put(slot + 1, ref[:piece], ref[piece:])

    def run(count):
        keys = count * piece
        lane = lax.broadcasted_iota(jnp.int32, (piece, piece), 1)
        row = lax.broadcasted_iota(jnp.int32, (piece, piece), 0)
        low = jnp.maximum(jnp.where(row >= cut, cut, -keys), -me * piece)
        caps = [
            jnp.where((lane - n * piece <= row) & (lane - n * piece >= low), jnp.inf, -jnp.inf) for n in range(count)
        ]
        cap = jnp.concatenate([jnp.concatenate(caps, axis=1)] * GROUP, axis=0)
        logs = jnp.zeros((piece, piece), jnp.float32)

        def scores(g):
            q = q_ref[0, g * GROUP:(g + 1) * GROUP].reshape(width, head)
            s = lax.dot_general(q, k_scr[:keys], (((1,), (1,)), ((), ())), preferred_element_type=jnp.float32)
            s = jnp.minimum(s, cap)
            return s, jnp.max(s, axis=1, keepdims=True)

        def weigh(s, m):
            p = jnp.exp2((s - m) * (scale * LOG2E))
            return p.astype(jnp.bfloat16), m, jnp.sum(p, axis=1, keepdims=True)

        def finish(g, logs, p, m, l):
            o = jnp.dot(p, v_scr[:keys], preferred_element_type=jnp.float32) * (1.0 / l)
            o_ref[0, g * GROUP:(g + 1) * GROUP] = o.astype(jnp.bfloat16).reshape(GROUP, piece, head)
            e = m * scale + jnp.log(l)
            for j in range(GROUP):
                logs = jnp.where(lane == g * GROUP + j, e[j * piece:(j + 1) * piece], logs)
            return logs

        groups = heads // GROUP
        now, before = scores(0), None
        for g in range(groups):
            later = scores(g + 1) if g + 1 < groups else None
            if before is not None:
                logs = finish(g - 1, logs, *before)
            before, now = weigh(*now), later
        logs = finish(groups - 1, logs, *before)
        lse_ref[:, pl.ds(seq, 1), :] = logs.T[:heads][:, None, :]

    for count in (2, 3, 4):
        @pl.when((need == count) | (count == 2 and need == 1))
        def _():
            run(count)


def attend(n, scalars, q, k, v, near, fara, farb, prev):
    batch, heads, piece, head = q.shape
    base, size = BOUNDS[n], CHUNKS[n]
    first = prev is None
    own = pl.BlockSpec((1, piece, head), lambda i: (base + i, 0, 0))
    whole = pl.BlockSpec((2 * piece, head), lambda i: (base + i, 0))
    chunk = pl.BlockSpec((2 * piece, head), lambda i: (i, 0))
    qspec = pl.BlockSpec((1, heads, piece, head), lambda i: (base + i, 0, 0, 0))
    lse = pl.BlockSpec((heads, batch, piece), lambda i: (0, 0, 0))
    in_specs = [pl.BlockSpec(memory_space=pltpu.SMEM), qspec, own, own, whole, chunk, chunk]
    args = [scalars, q, k, v, near, fara, farb]
    aliases = {}
    if not first:
        in_specs += [pl.BlockSpec(memory_space=pl.ANY), lse]
        args += list(prev)
        aliases = {7: 0}
    return pl.pallas_call(
        functools.partial(attend_kernel, first, base),
        grid=(size,),
        in_specs=in_specs,
        out_specs=[qspec, lse],
        scratch_shapes=[pltpu.VMEM((4 * piece, head), jnp.bfloat16)] * 2,
        out_shape=[
            jax.ShapeDtypeStruct(q.shape, jnp.bfloat16),
            jax.ShapeDtypeStruct((heads, batch, piece), jnp.float32),
        ],
        input_output_aliases=aliases,
        compiler_params=pltpu.CompilerParams(dimension_semantics=("arbitrary",)),
        cost_estimate=pl.CostEstimate(
            flops=size * heads * piece * 4 * piece * head * 4,
            bytes_accessed=size * heads * piece * head * 4,
            transcendentals=0,
        ),
    )(*args)


def shift(x, pairs):
    return lax.ppermute(x, "cp", pairs)


def solution(mesh):
    def local(q_loc, k_loc, v_loc, seg_loc):
        batch, piece, _, _ = q_loc.shape
        me = lax.axis_index("cp")
        q = jnp.transpose(q_loc, (0, 2, 1, 3))
        ranges = tuple(zip(BOUNDS[:-1], BOUNDS[1:]))
        sends = pack(ranges[:1], (True,), seg_loc, k_loc, v_loc)
        *more, whole = pack(ranges[1:] + ((0, batch),), (False,) * len(ranges[1:]) + (True,), seg_loc, k_loc, v_loc)
        sends = list(sends) + more
        fara = [shift(x, ACROSS) for x in sends]
        near = shift(whole, BESIDE)
        farb = [shift(x, SWAP) for x in fara]

        def zeros(packed, there):
            return jnp.where(there, packed[-batch:, 0].astype(jnp.int32), 0)

        odd, upper = me % 2 == 1, me >= 2
        cuts = zeros(whole, True) + zeros(near, odd) + zeros(fara[0], upper) + zeros(farb[0], upper)
        need = jnp.where(cuts <= me * piece, me - cuts // piece, me) + 1
        scalars = jnp.concatenate([
            jnp.stack([me, me % 2]).astype(jnp.int32), cuts - me * piece, need.astype(jnp.int32)
        ])
        state = None
        for n in range(len(CHUNKS)):
            state = attend(n, scalars, q, k_loc, v_loc, near, fara[n], farb[n], state)
        out, lse = state
        return jnp.transpose(out, (0, 2, 1, 3)), jnp.transpose(lse, (1, 2, 0))

    return jax.shard_map(
        local,
        mesh=mesh,
        in_specs=(P("dp", "cp", None, None), P("dp", "cp", None), P("dp", "cp", None), P("dp", "cp")),
        out_specs=(P("dp", "cp", None, None), P("dp", "cp", None)),
        check_vma=False,
    )
```

time: 186 us -> 170 us (0.914)
  waiting for transfers between devices: 36.7 us -> 73.8 us
  Pallas kernels: 79.6 us -> 60.8 us
  local copies, waits for them, and re-layouts: 16.1 us -> 1.04 us
  starting transfers between devices: 43.9 us -> 29.2 us
  other arithmetic: 7.25 us -> 1.49 us
    ppermute x21 -> x11, waiting for transfers between devices: 36.7 us -> 73.8 us  [shift(): return lax.ppermute(x, 'cp', pairs)]
    pallas_call x8 -> x7, Pallas kernels: 79.6 us -> 60.8 us  [the longest x5 52.2 us: attend(): pl.pallas_call(functools.partial(attend_kernel, first, base), grid=(size,...]
    ppermute x21 -> x11, starting transfers between devices: 43.9 us -> 29.2 us  [shift(): return lax.ppermute(x, 'cp', pairs)]
    slice x10 -> x0, local copies, waits for them, and re-layouts: 11.7 us -> none  [the longest x5 7.48 us: local(): k_loc[a:b]]
    concatenate x8 -> x1, other arithmetic: 6.81 us -> 0.6 us  [local(): jnp.concatenate([jnp.stack([me, me % 2]).astype(jnp.int32), cuts - me * p...]
    unnamed x48 -> x8, local copies, waits for them, and re-layouts: 3.78 us -> 1.04 us
  transfers between devices with their start and end apart: 21 -> 11, of which waited for: 7 -> 3; matrix products, arithmetic and copies ran while one was open for 11% -> 1% of each run, Pallas kernels for 41% -> 28%
where the time goes in v3:
time: 170 us; the launch traced here: 167 us
  waiting for transfers between devices  73.8 us (43%)
  Pallas kernels  60.8 us (36%)
  starting transfers between devices  29.2 us (17%)
    ppermute x11, waiting for transfers between devices, shift(): return lax.ppermute(x, 'cp', pairs)  73.8 us
    pallas_call x5, Pallas kernels, attend(): pl.pallas_call(functools.partial(attend_kernel, first, base), grid=(size,...  52.2 us
    ppermute x11, starting transfers between devices, shift(): return lax.ppermute(x, 'cp', pairs)  29.2 us
    pallas_call x2, Pallas kernels, pack(): pl.pallas_call(functools.partial(pack_kernel, ranges, tails), in_specs=[p...  8.64 us
  transfers between devices with their start and end apart: 11, of which 3 were waited for; matrix products, arithmetic and copies ran while one was open for 1% of the time, Pallas kernels for 28%

profile of v3, /device:TPU:7, one launch (start us, length us, event | category | flops | bytes accessed | tf_op | source)
XLA Modules:
  0.0 167.3 jit_solution(8249953778228245838)
XLA Ops:
  0.6 6.0 %shard_map.59 = (bf16[2048,256]{1,0:T(8,128)(2,1)}, bf16[2048,256]{1,0:T(8,128)(2,1)}, bf16[1792,256]{1,0:T(8,128)(2,1)}, bf16[1280,256]{1,0:T(8,128)(2,1)}, bf16[8224,256]{1,0:T(8,128)(2,1)}) custom-call(s32[32,128]{1,0:T(8,128)} %seg_ref.3, bf16[32,128,256]{2,1,0:T(8,128)(2,1)} %k_ref.13, bf16[32,128,256]{2,1,0:T(8,128)(2,1)} %v_ref.13), custom_call_target="tpu_custom_call" | custom-call | flops 1048576 | bytes 4194304 | tf_op jit(solution)/shard_map/pallas_call | solution.py:53
  6.7 1.3 collective-permute-start
  8.0 2.6 %shard_map.60 = bf16[1056,256]{1,0:T(8,128)(2,1)} custom-call(s32[32,128]{1,0:T(8,128)} %seg_ref.3, bf16[32,128,256]{2,1,0:T(8,128)(2,1)} %k_ref.13, bf16[32,128,256]{2,1,0:T(8,128)(2,1)} %v_ref.13), custom_call_target="tpu_custom_call" | custom-call | flops 1048576 | bytes 4194304 | tf_op jit(solution)/shard_map/pallas_call | solution.py:53
  10.6 1.3 collective-permute-start.1
  11.9 1.3 collective-permute-start.9
  13.2 1.3 collective-permute-start.3
  14.5 1.3 collective-permute-start.7
  15.8 7.8 %collective-permute-done.1.fara_ref = bf16[1056,256]{1,0:T(8,128)(2,1)} collective-permute-done((bf16[1056,256]{1,0:T(8,128)(2,1)}, bf16[1056,256]{1,0:T(8,128)(2,1)}, u32[]{:S(2)}, u32[]{:S(2)}) %collective-permute-start.1) | collective-permute-done | bytes 540704 | tf_op jit(solution)/shard_map/ppermute | solution.py:189
  23.5 1.3 collective-permute-start.5
  24.8 35.1 %collective-permute-done.3.fara_ref = bf16[1280,256]{1,0:T(8,128)(2,1)S(1)} collective-permute-done((bf16[1280,256]{1,0:T(8,128)(2,1)}, bf16[1280,256]{1,0:T(8,128)(2,1)S(1)}, u32[]{:S(2)}, u32[]{:S(2)}) %collective-permute-start.3) | collective-permute-done | bytes 655392 | tf_op jit(solution)/shard_map/ppermute | solution.py:189
  60.0 0.0 copy-start.3
  60.0 9.4 %collective-permute-start.2 = (bf16[1056,256]{1,0:T(8,128)(2,1)}, bf16[1056,256]{1,0:T(8,128)(2,1)}, u32[]{:S(2)}, u32[]{:S(2)}) collective-permute-start(bf16[1056,256]{1,0:T(8,128)(2,1)} %collective-permute-done.1.fara_ref), channel_id=1, source_target_pairs={{2,3},{3,2},{6,7},{7,6}} | collective-permute-start | bytes 1622024 | tf_op jit(solution)/shard_map/ppermute | solution.py:189
  69.3 0.0 copy-done.3
  69.3 0.0 collective-permute-done.9.fara_ref
  69.4 0.0 copy-start.1
  69.4 1.9 %collective-permute-start.10 = (bf16[2048,256]{1,0:T(8,128)(2,1)S(1)}, bf16[2048,256]{1,0:T(8,128)(2,1)S(1)}, u32[]{:S(2)}, u32[]{:S(2)}) collective-permute-start(bf16[2048,256]{1,0:T(8,128)(2,1)S(1)} %collective-permute-done.9.fara_ref), channel_id=1, source_target_pairs={{2,3},{3,2},{6,7},{7,6}} | collective-permute-start | bytes 3145736 | tf_op jit(solution)/shard_map/ppermute | solution.py:189
  71.3 30.9 %collective-permute-done.5.fara_ref = bf16[1792,256]{1,0:T(8,128)(2,1)} collective-permute-done((bf16[1792,256]{1,0:T(8,128)(2,1)}, bf16[1792,256]{1,0:T(8,128)(2,1)}, u32[]{:S(2)}, u32[]{:S(2)}) %collective-permute-start.5) | collective-permute-done | bytes 917536 | tf_op jit(solution)/shard_map/ppermute | solution.py:189
  102.2 5.8 %collective-permute-start.4 = (bf16[1280,256]{1,0:T(8,128)(2,1)}, bf16[1280,256]{1,0:T(8,128)(2,1)}, u32[]{:S(2)}, u32[]{:S(2)}) collective-permute-start(bf16[1280,256]{1,0:T(8,128)(2,1)} %copy-done.3), channel_id=1, source_target_pairs={{2,3},{3,2},{6,7},{7,6}} | collective-permute-start | bytes 1966088 | tf_op jit(solution)/shard_map/ppermute | solution.py:189
  108.0 0.0 collective-permute-done.7.fara_ref
  108.0 0.0 copy-start
  108.1 1.9 %collective-permute-start.6 = (bf16[1792,256]{1,0:T(8,128)(2,1)}, bf16[1792,256]{1,0:T(8,128)(2,1)}, u32[]{:S(2)}, u32[]{:S(2)}) collective-permute-start(bf16[1792,256]{1,0:T(8,128)(2,1)} %collective-permute-done.5.fara_ref), channel_id=1, source_target_pairs={{2,3},{3,2},{6,7},{7,6}} | collective-permute-start | bytes 2752520 | tf_op jit(solution)/shard_map/ppermute | solution.py:189
  110.0 0.0 collective-permute-done.2.farb_ref
  110.0 2.4 %collective-permute-start.8 = (bf16[2048,256]{1,0:T(8,128)(2,1)S(1)}, bf16[2048,256]{1,0:T(8,128)(2,1)}, u32[]{:S(2)}, u32[]{:S(2)}) collective-permute-start(bf16[2048,256]{1,0:T(8,128)(2,1)S(1)} %collective-permute-done.7.fara_ref), channel_id=1, source_target_pairs={{2,3},{3,2},{6,7},{7,6}} | collective-permute-start | bytes 3145736 | tf_op jit(solution)/shard_map/ppermute | solution.py:189
  112.4 0.0 collective-permute-done.near_ref
  112.4 0.9 add_reduce_fusion
  113.3 0.6 pad_add_fusion.s_ref
  113.9 7.2 %shard_map.61 = (bf16[32,10,128,256]{3,2,1,0:T(8,128)(2,1)}, f32[10,32,128]{2,1,0:T(8,128)}) custom-call(s32[66]{0:T(128)} %pad_add_fusion.s_ref, bf16[32,10,128,256]{3,2,1,0:T(8,128)(2,1)} %bitcast.5, bf16[32,128,256]{2,1,0:T(8,128)(2,1)} %k_ref.13, bf16[32,128,256]{2,1,0:T(8,128)(2,1)} %v_ref.13, bf16[8224,256]{1,0:T(8,128)(2,1)} %collective-permute-done.near_ref, ...), custom_call_target="tpu_custom_call" | custom-call | flops 2684354560 | bytes 5242880 | tf_op jit(solution)/shard_map/pallas_call | solution.py:168
  121.1 0.0 collective-permute-done.10.farb_ref
  121.1 0.0 copy-start.2
  121.2 0.0 copy-done.1
  121.2 1.0 copy-done.2
  122.2 13.4 %shard_map.62 = (bf16[32,10,128,256]{3,2,1,0:T(8,128)(2,1)}, f32[10,32,128]{2,1,0:T(8,128)}) custom-call(s32[66]{0:T(128)} %pad_add_fusion.s_ref, bf16[32,10,128,256]{3,2,1,0:T(8,128)(2,1)} %bitcast.6, bf16[32,128,256]{2,1,0:T(8,128)(2,1)} %k_ref.13, bf16[32,128,256]{2,1,0:T(8,128)(2,1)} %v_ref.13, ...), custom_call_target="tpu_custom_call", output_to_operand_aliasing={{0}: (7, {})} | custom-call | flops 5368709120 | bytes 10485760 | tf_op jit(solution)/shard_map/pallas_call | solution.py:168
  135.6 0.0 copy-done
  135.6 0.0 collective-permute-done.8.farb_ref
  135.6 12.5 %shard_map.63 = (bf16[32,10,128,256]{3,2,1,0:T(8,128)(2,1)}, f32[10,32,128]{2,1,0:T(8,128)}) custom-call(s32[66]{0:T(128)} %pad_add_fusion.s_ref, bf16[32,10,128,256]{3,2,1,0:T(8,128)(2,1)} %bitcast.7, bf16[32,128,256]{2,1,0:T(8,128)(2,1)} %k_ref.13, bf16[32,128,256]{2,1,0:T(8,128)(2,1)} %v_ref.13, ...), custom_call_target="tpu_custom_call", output_to_operand_aliasing={{0}: (7, {})} | custom-call | flops 5368709120 | bytes 10485760 | tf_op jit(solution)/shard_map/pallas_call | solution.py:168
  148.1 0.0 collective-permute-done.6.farb_ref
  148.1 11.1 %shard_map.64 = (bf16[32,10,128,256]{3,2,1,0:T(8,128)(2,1)}, f32[10,32,128]{2,1,0:T(8,128)}) custom-call(s32[66]{0:T(128)} %pad_add_fusion.s_ref, bf16[32,10,128,256]{3,2,1,0:T(8,128)(2,1)} %bitcast.8, bf16[32,128,256]{2,1,0:T(8,128)(2,1)} %k_ref.13, bf16[32,128,256]{2,1,0:T(8,128)(2,1)} %v_ref.13, ...), custom_call_target="tpu_custom_call", output_to_operand_aliasing={{0}: (7, {})} | custom-call | flops 4697620480 | bytes 9175040 | tf_op jit(solution)/shard_map/pallas_call | solution.py:168
  159.3 0.0 collective-permute-done.4.farb_ref
  159.3 7.9 %shard_map.65 = (bf16[32,10,128,256]{3,2,1,0:T(8,128)(2,1)}, f32[10,32,128]{2,1,0:T(8,128)}) custom-call(s32[66]{0:T(128)} %pad_add_fusion.s_ref, bf16[32,10,128,256]{3,2,1,0:T(8,128)(2,1)} %bitcast.9, bf16[32,128,256]{2,1,0:T(8,128)(2,1)} %k_ref.13, bf16[32,128,256]{2,1,0:T(8,128)(2,1)} %v_ref.13, ...), custom_call_target="tpu_custom_call", output_to_operand_aliasing={{0}: (7, {})} | custom-call | flops 3355443200 | bytes 6553600 | tf_op jit(solution)/shard_map/pallas_call | solution.py:168
  (1 shorter events, 0.0 us)
Async XLA Ops:
  6.7 105.8 %collective-permute-start = (bf16[8224,256]{1,0:T(8,128)(2,1)}, bf16[8224,256]{1,0:T(8,128)(2,1)}, u32[]{:S(2)}, u32[]{:S(2)}) collective-permute-start(bf16[8224,256]{1,0:T(8,128)(2,1)} %get-tuple-element.17), channel_id=1, source_target_pairs={{0,1},{2,3},{4,5},{6,7}} | collective-permute-start | bytes 12632072 | tf_op jit(solution)/shard_map/ppermute | solution.py:189
  10.6 13.0 %collective-permute-start.1 = (bf16[1056,256]{1,0:T(8,128)(2,1)}, bf16[1056,256]{1,0:T(8,128)(2,1)}, u32[]{:S(2)}, u32[]{:S(2)}) collective-permute-start(bf16[1056,256]{1,0:T(8,128)(2,1)} %shard_map.60), channel_id=1, source_target_pairs={{0,2},{1,3},{4,6},{5,7}} | collective-permute-start | bytes 1622024 | tf_op jit(solution)/shard_map/ppermute | solution.py:189
  11.9 57.5 %collective-permute-start.9 = (bf16[2048,256]{1,0:T(8,128)(2,1)}, bf16[2048,256]{1,0:T(8,128)(2,1)S(1)}, u32[]{:S(2)}, u32[]{:S(2)}) collective-permute-start(bf16[2048,256]{1,0:T(8,128)(2,1)} %get-tuple-element.21), channel_id=1, source_target_pairs={{0,2},{1,3},{4,6},{5,7}} | collective-permute-start | bytes 3145736 | tf_op jit(solution)/shard_map/ppermute | solution.py:189
  13.2 46.8 %collective-permute-start.3 = (bf16[1280,256]{1,0:T(8,128)(2,1)}, bf16[1280,256]{1,0:T(8,128)(2,1)S(1)}, u32[]{:S(2)}, u32[]{:S(2)}) collective-permute-start(bf16[1280,256]{1,0:T(8,128)(2,1)} %get-tuple-element.18), channel_id=1, source_target_pairs={{0,2},{1,3},{4,6},{5,7}} | collective-permute-start | bytes 1966088 | tf_op jit(solution)/shard_map/ppermute | solution.py:189
  14.5 93.6 %collective-permute-start.7 = (bf16[2048,256]{1,0:T(8,128)(2,1)}, bf16[2048,256]{1,0:T(8,128)(2,1)S(1)}, u32[]{:S(2)}, u32[]{:S(2)}) collective-permute-start(bf16[2048,256]{1,0:T(8,128)(2,1)} %get-tuple-element.20), channel_id=1, source_target_pairs={{0,2},{1,3},{4,6},{5,7}} | collective-permute-start | bytes 3145736 | tf_op jit(solution)/shard_map/ppermute | solution.py:189
  23.5 78.6 %collective-permute-start.5 = (bf16[1792,256]{1,0:T(8,128)(2,1)}, bf16[1792,256]{1,0:T(8,128)(2,1)}, u32[]{:S(2)}, u32[]{:S(2)}) collective-permute-start(bf16[1792,256]{1,0:T(8,128)(2,1)} %get-tuple-element.19), channel_id=1, source_target_pairs={{0,2},{1,3},{4,6},{5,7}} | collective-permute-start | bytes 2752520 | tf_op jit(solution)/shard_map/ppermute | solution.py:189
  60.0 9.4 %copy-start.3 = (bf16[1280,256]{1,0:T(8,128)(2,1)}, bf16[1280,256]{1,0:T(8,128)(2,1)S(1)}, u32[]{:S(2)}) copy-start(bf16[1280,256]{1,0:T(8,128)(2,1)S(1)} %collective-permute-done.3.fara_ref) | copy-start | bytes 1966084
  60.0 50.0 %collective-permute-start.2 = (bf16[1056,256]{1,0:T(8,128)(2,1)}, bf16[1056,256]{1,0:T(8,128)(2,1)}, u32[]{:S(2)}, u32[]{:S(2)}) collective-permute-start(bf16[1056,256]{1,0:T(8,128)(2,1)} %collective-permute-done.1.fara_ref), channel_id=1, source_target_pairs={{2,3},{3,2},{6,7},{7,6}} | collective-permute-start | bytes 1622024 | tf_op jit(solution)/shard_map/ppermute | solution.py:189
  69.4 51.8 %copy-start.1 = (bf16[2048,256]{1,0:T(8,128)(2,1)}, bf16[2048,256]{1,0:T(8,128)(2,1)S(1)}, u32[]{:S(2)}) copy-start(bf16[2048,256]{1,0:T(8,128)(2,1)S(1)} %collective-permute-done.9.fara_ref) | copy-start | bytes 3145732
  69.4 51.8 %collective-permute-start.10 = (bf16[2048,256]{1,0:T(8,128)(2,1)S(1)}, bf16[2048,256]{1,0:T(8,128)(2,1)S(1)}, u32[]{:S(2)}, u32[]{:S(2)}) collective-permute-start(bf16[2048,256]{1,0:T(8,128)(2,1)S(1)} %collective-permute-done.9.fara_ref), channel_id=1, source_target_pairs={{2,3},{3,2},{6,7},{7,6}} | collective-permute-start | bytes 3145736 | tf_op jit(solution)/shard_map/ppermute | solution.py:189
  102.2 57.1 %collective-permute-start.4 = (bf16[1280,256]{1,0:T(8,128)(2,1)}, bf16[1280,256]{1,0:T(8,128)(2,1)}, u32[]{:S(2)}, u32[]{:S(2)}) collective-permute-start(bf16[1280,256]{1,0:T(8,128)(2,1)} %copy-done.3), channel_id=1, source_target_pairs={{2,3},{3,2},{6,7},{7,6}} | collective-permute-start | bytes 1966088 | tf_op jit(solution)/shard_map/ppermute | solution.py:189
  108.0 27.6 %copy-start = (bf16[2048,256]{1,0:T(8,128)(2,1)}, bf16[2048,256]{1,0:T(8,128)(2,1)S(1)}, u32[]{:S(2)}) copy-start(bf16[2048,256]{1,0:T(8,128)(2,1)S(1)} %collective-permute-done.7.fara_ref) | copy-start | bytes 3145732
  108.1 40.0 %collective-permute-start.6 = (bf16[1792,256]{1,0:T(8,128)(2,1)}, bf16[1792,256]{1,0:T(8,128)(2,1)}, u32[]{:S(2)}, u32[]{:S(2)}) collective-permute-start(bf16[1792,256]{1,0:T(8,128)(2,1)} %collective-permute-done.5.fara_ref), channel_id=1, source_target_pairs={{2,3},{3,2},{6,7},{7,6}} | collective-permute-start | bytes 2752520 | tf_op jit(solution)/shard_map/ppermute | solution.py:189
  110.0 25.6 %collective-permute-start.8 = (bf16[2048,256]{1,0:T(8,128)(2,1)S(1)}, bf16[2048,256]{1,0:T(8,128)(2,1)}, u32[]{:S(2)}, u32[]{:S(2)}) collective-permute-start(bf16[2048,256]{1,0:T(8,128)(2,1)S(1)} %collective-permute-done.7.fara_ref), channel_id=1, source_target_pairs={{2,3},{3,2},{6,7},{7,6}} | collective-permute-start | bytes 3145736 | tf_op jit(solution)/shard_map/ppermute | solution.py:189
  121.1 1.0 copy-start.2

commit v4 on v3

--- a/solution.py
+++ b/solution.py
@@ -8,9 +8,10 @@
 from jax.sharding import PartitionSpec as P
 
 
-CHUNKS = (4, 8, 8, 7, 5)
+CHUNKS = (4, 8, 8, 7, 3, 2)
 BOUNDS = tuple(sum(CHUNKS[:n]) for n in range(len(CHUNKS) + 1))
 GROUP = 2
+DEPTH = 4
 LOG2E = 1.4426950408889634
 
 ACROSS = [(0, 2), (1, 3)]
@@ -69,42 +70,44 @@
     )(seg, k, v)
 
 
-def attend_kernel(first, base, s_ref, q_ref, k_ref, v_ref, near_ref, fara_ref, farb_ref, *rest):
+def attend_kernel(first, base, size, s_ref, q_ref, k_ref, v_ref, near_ref, fara_ref, farb_ref, *rest):
     if first:
-        o_ref, lse_ref, k_scr, v_scr = rest
+        o_ref, lse_ref, q_buf, k_buf, v_buf, o_buf, in_sem, out_sem = rest
     else:
-        _, lse_in, o_ref, lse_ref, k_scr, v_scr = rest
-    step = pl.program_id(0)
-    seq = base + step
-    heads, piece, head = q_ref.shape[1:]
+        _, lse_in, o_ref, lse_ref, q_buf, k_buf, v_buf, o_buf, in_sem, out_sem = rest
+        lse_ref[...] = lse_in[...]
+    depth, heads, piece, head = q_buf.shape
     batch = lse_ref.shape[1]
     width = GROUP * piece
     scale = head ** -0.5
     me, odd = s_ref[0], s_ref[1]
-    cut, need = s_ref[2 + seq], s_ref[2 + batch + seq]
-
-    if not first:
-        @pl.when(step == 0)
-        def _():
-            lse_ref[...] = lse_in[...]
-
-    def put(slot, k, v):
-        k_scr[slot * piece:(slot + 1) * piece] = k
-        v_scr[slot * piece:(slot + 1) * piece] = v
-
-    put(0, k_ref[0], v_ref[0])
-
-    @pl.when(odd == 1)
-    def _():
-        for slot, ref in enumerate((near_ref, fara_ref, farb_ref)):
-            put(slot + 1, ref[:piece], ref[piece:])
-
-    @pl.when(odd == 0)
-    def _():
-        for slot, ref in enumerate((farb_ref, fara_ref)):
-            put(slot + 1, ref[:piece], ref[piece:])
-
-    def run(count):
+
+    def loads(step):
+        slot = lax.rem(step, depth)
+        seq = base + step
+        out = [
+            pltpu.make_async_copy(q_ref.at[seq], q_buf.at[slot], in_sem.at[slot]),
+            pltpu.make_async_copy(k_ref.at[seq], k_buf.at[slot, pl.ds(0, piece)], in_sem.at[slot]),
+            pltpu.make_async_copy(v_ref.at[seq], v_buf.at[slot, pl.ds(0, piece)], in_sem.at[slot]),
+        ]
+        there = pl.ds(pl.multiple_of(jnp.where(odd == 1, 1, 3) * piece, piece), piece)
+        for half, buf in enumerate((k_buf, v_buf)):
+            rows = pl.ds(pl.multiple_of((2 * seq + half) * piece, piece), piece)
+            out.append(pltpu.make_async_copy(near_ref.at[rows], buf.at[slot, there], in_sem.at[slot]))
+        return out
+
+    def place(step):
+        slot = lax.rem(step, depth)
+        for ref, block in ((fara_ref, 2), (farb_ref, jnp.where(odd == 1, 3, 1))):
+            there = pl.ds(pl.multiple_of(block * piece, piece), piece)
+            for half, buf in enumerate((k_buf, v_buf)):
+                buf[slot, there] = ref[pl.ds(pl.multiple_of((2 * step + half) * piece, piece), piece)]
+
+    def store(step):
+        slot = lax.rem(step, 2)
+        return pltpu.make_async_copy(o_buf.at[slot], o_ref.at[base + step], out_sem.at[slot])
+
+    def run(count, seq, slot, out, cut):
         keys = count * piece
         lane = lax.broadcasted_iota(jnp.int32, (piece, piece), 1)
         row = lax.broadcasted_iota(jnp.int32, (piece, piece), 0)
@@ -116,8 +119,8 @@
         logs = jnp.zeros((piece, piece), jnp.float32)
 
         def scores(g):
-            q = q_ref[0, g * GROUP:(g + 1) * GROUP].reshape(width, head)
-            s = lax.dot_general(q, k_scr[:keys], (((1,), (1,)), ((), ())), preferred_element_type=jnp.float32)
+            q = q_buf[slot, g * GROUP:(g + 1) * GROUP].reshape(width, head)
+            s = lax.dot_general(q, k_buf[slot, :keys], (((1,), (1,)), ((), ())), preferred_element_type=jnp.float32)
             s = jnp.minimum(s, cap)
             return s, jnp.max(s, axis=1, keepdims=True)
 
@@ -126,8 +129,8 @@
             return p.astype(jnp.bfloat16), m, jnp.sum(p, axis=1, keepdims=True)
 
         def finish(g, logs, p, m, l):
-            o = jnp.dot(p, v_scr[:keys], preferred_element_type=jnp.float32) * (1.0 / l)
-            o_ref[0, g * GROUP:(g + 1) * GROUP] = o.astype(jnp.bfloat16).reshape(GROUP, piece, head)
+            o = jnp.dot(p, v_buf[slot, :keys], preferred_element_type=jnp.float32) * (1.0 / l)
+            o_buf[out, g * GROUP:(g + 1) * GROUP] = o.astype(jnp.bfloat16).reshape(GROUP, piece, head)
             e = m * scale + jnp.log(l)
             for j in range(GROUP):
                 logs = jnp.where(lane == g * GROUP + j, e[j * piece:(j + 1) * piece], logs)
@@ -143,40 +146,69 @@
         logs = finish(groups - 1, logs, *before)
         lse_ref[:, pl.ds(seq, 1), :] = logs.T[:heads][:, None, :]
 
-    for count in (2, 3, 4):
-        @pl.when((need == count) | (count == 2 and need == 1))
+    for step in range(min(depth - 1, size)):
+        for load in loads(step):
+            load.start()
+
+    @pl.loop(0, size)
+    def _(step):
+        seq = base + step
+
+        @pl.when(step + depth - 1 < size)
         def _():
-            run(count)
+            for load in loads(step + depth - 1):
+                load.start()
+
+        @pl.when(step >= 2)
+        def _():
+            store(step - 2).wait()
+
+        for load in loads(step):
+            load.wait()
+        place(step)
+        cut, need = s_ref[2 + seq], s_ref[2 + batch + seq]
+        for count in (2, 3, 4):
+            @pl.when((need == count) | (count == 2 and need == 1))
+            def _():
+                run(count, seq, lax.rem(step, depth), lax.rem(step, 2), cut)
+        store(step).start()
+
+    for step in range(max(size - 2, 0), size):
+        store(step).wait()
 
 
 def attend(n, scalars, q, k, v, near, fara, farb, prev):
     batch, heads, piece, head = q.shape
     base, size = BOUNDS[n], CHUNKS[n]
     first = prev is None
-    own = pl.BlockSpec((1, piece, head), lambda i: (base + i, 0, 0))
-    whole = pl.BlockSpec((2 * piece, head), lambda i: (base + i, 0))
-    chunk = pl.BlockSpec((2 * piece, head), lambda i: (i, 0))
-    qspec = pl.BlockSpec((1, heads, piece, head), lambda i: (base + i, 0, 0, 0))
-    lse = pl.BlockSpec((heads, batch, piece), lambda i: (0, 0, 0))
-    in_specs = [pl.BlockSpec(memory_space=pltpu.SMEM), qspec, own, own, whole, chunk, chunk]
+    hbm = pl.BlockSpec(memory_space=pltpu.HBM)
+    vmem = pl.BlockSpec(memory_space=pltpu.VMEM)
+    in_specs = [pl.BlockSpec(memory_space=pltpu.SMEM)] + [hbm] * 4 + [vmem] * 2
+    q, k, v, near = (pltpu.with_memory_space_constraint(x, pltpu.HBM) for x in (q, k, v, near))
     args = [scalars, q, k, v, near, fara, farb]
     aliases = {}
     if not first:
-        in_specs += [pl.BlockSpec(memory_space=pl.ANY), lse]
+        in_specs += [hbm, vmem]
         args += list(prev)
         aliases = {7: 0}
     return pl.pallas_call(
-        functools.partial(attend_kernel, first, base),
-        grid=(size,),
+        functools.partial(attend_kernel, first, base, size),
         in_specs=in_specs,
-        out_specs=[qspec, lse],
-        scratch_shapes=[pltpu.VMEM((4 * piece, head), jnp.bfloat16)] * 2,
+        out_specs=[hbm, vmem],
+        scratch_shapes=[
+            pltpu.VMEM((DEPTH, heads, piece, head), jnp.bfloat16),
+            pltpu.VMEM((DEPTH, 4 * piece, head), jnp.bfloat16),
+            pltpu.VMEM((DEPTH, 4 * piece, head), jnp.bfloat16),
+            pltpu.VMEM((2, heads, piece, head), jnp.bfloat16),
+            pltpu.SemaphoreType.DMA((DEPTH,)),
+            pltpu.SemaphoreType.DMA((2,)),
+        ],
         out_shape=[
             jax.ShapeDtypeStruct(q.shape, jnp.bfloat16),
             jax.ShapeDtypeStruct((heads, batch, piece), jnp.float32),
         ],
         input_output_aliases=aliases,
-        compiler_params=pltpu.CompilerParams(dimension_semantics=("arbitrary",)),
+        compiler_params=pltpu.CompilerParams(vmem_limit_bytes=32 << 20),
         cost_estimate=pl.CostEstimate(
             flops=size * heads * piece * 4 * piece * head * 4,
             bytes_accessed=size * heads * piece * head * 4,

time: 170 us -> 168 us (0.988)
  waiting for transfers between devices: 73.8 us -> 69.3 us
  starting transfers between devices: 29.2 us -> 32.3 us
    ppermute x11 -> x13, waiting for transfers between devices: 73.8 us -> 69.3 us  [shift(): return lax.ppermute(x, 'cp', pairs)]
    ppermute x11 -> x13, starting transfers between devices: 29.2 us -> 32.3 us  [shift(): return lax.ppermute(x, 'cp', pairs)]
    pallas_call x5 -> x6, Pallas kernels: 52.2 us -> 52.9 us  [attend(): pl.pallas_call(functools.partial(attend_kernel, first, base, size), in_sp...]
  transfers between devices with their start and end apart: 11 -> 13, of which waited for: 3 -> 3; matrix products, arithmetic and copies ran while one was open for 1% -> 1% of each run, Pallas kernels for 28% -> 30%
where the time goes in v4:
time: 168 us; the launch traced here: 166 us
  waiting for transfers between devices  69.3 us (41%)
  Pallas kernels  61.5 us (37%)
  starting transfers between devices  32.3 us (19%)
    ppermute x13, waiting for transfers between devices, shift(): return lax.ppermute(x, 'cp', pairs)  69.3 us
    pallas_call x6, Pallas kernels, attend(): pl.pallas_call(functools.partial(attend_kernel, first, base, size), in_sp...  52.9 us
    ppermute x13, starting transfers between devices, shift(): return lax.ppermute(x, 'cp', pairs)  32.3 us
    pallas_call x2, Pallas kernels, pack(): pl.pallas_call(functools.partial(pack_kernel, ranges, tails), in_specs=[p...  8.63 us
  transfers between devices with their start and end apart: 13, of which 3 were waited for; matrix products, arithmetic and copies ran while one was open for 1% of the time, Pallas kernels for 30%

profile of v4, /device:TPU:7, one launch (start us, length us, event | category | flops | bytes accessed | tf_op | source)
XLA Modules:
  0.0 165.8 jit_solution(4978551900235340741)
XLA Ops:
  0.6 6.0 %shard_map.59 = (bf16[2048,256]{1,0:T(8,128)(2,1)}, bf16[2048,256]{1,0:T(8,128)(2,1)}, bf16[1792,256]{1,0:T(8,128)(2,1)}, bf16[768,256]{1,0:T(8,128)(2,1)}, bf16...) custom-call(s32[32,128]{1,0:T(8,128)} %seg_ref.3, bf16[32,128,256]{2,1,0:T(8,128)(2,1)} %k_ref.15, ...), custom_call_target="tpu_custom_call" | custom-call | flops 1048576 | bytes 4194304 | tf_op jit(solution)/shard_map/pallas_call | solution.py:54
  6.7 1.3 collective-permute-start
  8.0 1.3 collective-permute-start.11
  9.3 1.3 collective-permute-start.5
  10.6 1.3 collective-permute-start.3
  11.9 2.6 %shard_map.60 = bf16[1056,256]{1,0:T(8,128)(2,1)} custom-call(s32[32,128]{1,0:T(8,128)} %seg_ref.3, bf16[32,128,256]{2,1,0:T(8,128)(2,1)} %k_ref.15, bf16[32,128,256]{2,1,0:T(8,128)(2,1)} %v_ref.15), custom_call_target="tpu_custom_call" | custom-call | flops 1048576 | bytes 4194304 | tf_op jit(solution)/shard_map/pallas_call | solution.py:54
  14.5 1.3 collective-permute-start.1
  15.8 30.0 %collective-permute-done.3.fara_ref = bf16[512,256]{1,0:T(8,128)(2,1)S(1)} collective-permute-done((bf16[512,256]{1,0:T(8,128)(2,1)}, bf16[512,256]{1,0:T(8,128)(2,1)S(1)}, u32[]{:S(2)}, u32[]{:S(2)}) %collective-permute-start.3) | collective-permute-done | bytes 262176 | tf_op jit(solution)/shard_map/ppermute | solution.py:221
  45.8 0.0 copy-start
  45.8 0.7 copy-done
  46.4 1.3 collective-permute-start.9
  47.7 0.0 collective-permute-done.5.fara_ref
  47.7 1.3 collective-permute-start.7
  49.0 8.4 %collective-permute-done.1.fara_ref = bf16[1056,256]{1,0:T(8,128)(2,1)} collective-permute-done((bf16[1056,256]{1,0:T(8,128)(2,1)}, bf16[1056,256]{1,0:T(8,128)(2,1)}, u32[]{:S(2)}, u32[]{:S(2)}) %collective-permute-start.1) | collective-permute-done | bytes 540704 | tf_op jit(solution)/shard_map/ppermute | solution.py:221
  57.4 9.3 %collective-permute-start.2 = (bf16[1056,256]{1,0:T(8,128)(2,1)}, bf16[1056,256]{1,0:T(8,128)(2,1)}, u32[]{:S(2)}, u32[]{:S(2)}) collective-permute-start(bf16[1056,256]{1,0:T(8,128)(2,1)} %collective-permute-done.1.fara_ref), channel_id=1, source_target_pairs={{2,3},{3,2},{6,7},{7,6}} | collective-permute-start | bytes 1622024 | tf_op jit(solution)/shard_map/ppermute | solution.py:221
  66.8 0.0 collective-permute-done.11.fara_ref
  66.8 1.9 %collective-permute-start.12 = (bf16[2048,256]{1,0:T(8,128)(2,1)S(1)}, bf16[2048,256]{1,0:T(8,128)(2,1)S(1)}, u32[]{:S(2)}, u32[]{:S(2)}) collective-permute-start(bf16[2048,256]{1,0:T(8,128)(2,1)S(1)} %collective-permute-done.11.fara_ref), channel_id=1, source_target_pairs={{2,3},{3,2},{6,7},{7,6}} | collective-permute-start | bytes 3145736 | tf_op jit(solution)/shard_map/ppermute | solution.py:221
  68.7 30.8 %collective-permute-done.7.fara_ref = bf16[1792,256]{1,0:T(8,128)(2,1)} collective-permute-done((bf16[1792,256]{1,0:T(8,128)(2,1)}, bf16[1792,256]{1,0:T(8,128)(2,1)}, u32[]{:S(2)}, u32[]{:S(2)}) %collective-permute-start.7) | collective-permute-done | bytes 917536 | tf_op jit(solution)/shard_map/ppermute | solution.py:221
  99.6 5.8 %collective-permute-start.4 = (bf16[512,256]{1,0:T(8,128)(2,1)}, bf16[512,256]{1,0:T(8,128)(2,1)S(1)}, u32[]{:S(2)}, u32[]{:S(2)}) collective-permute-start(bf16[512,256]{1,0:T(8,128)(2,1)} %copy-done), channel_id=1, source_target_pairs={{2,3},{3,2},{6,7},{7,6}} | collective-permute-start | bytes 786440 | tf_op jit(solution)/shard_map/ppermute | solution.py:221
  105.4 0.0 collective-permute-done.9.fara_ref
  105.4 1.9 %collective-permute-start.6 = (bf16[768,256]{1,0:T(8,128)(2,1)S(1)}, bf16[768,256]{1,0:T(8,128)(2,1)S(1)}, u32[]{:S(2)}, u32[]{:S(2)}) collective-permute-start(bf16[768,256]{1,0:T(8,128)(2,1)S(1)} %collective-permute-done.5.fara_ref), channel_id=1, source_target_pairs={{2,3},{3,2},{6,7},{7,6}} | collective-permute-start | bytes 1179656 | tf_op jit(solution)/shard_map/ppermute | solution.py:221
  107.3 0.0 collective-permute-done.2.farb_ref
  107.4 2.4 %collective-permute-start.8 = (bf16[1792,256]{1,0:T(8,128)(2,1)}, bf16[1792,256]{1,0:T(8,128)(2,1)S(1)}, u32[]{:S(2)}, u32[]{:S(2)}) collective-permute-start(bf16[1792,256]{1,0:T(8,128)(2,1)} %collective-permute-done.7.fara_ref), channel_id=1, source_target_pairs={{2,3},{3,2},{6,7},{7,6}} | collective-permute-start | bytes 2752520 | tf_op jit(solution)/shard_map/ppermute | solution.py:221
  109.8 0.0 collective-permute-done.near_ref
  109.8 1.9 %collective-permute-start.10 = (bf16[2048,256]{1,0:T(8,128)(2,1)S(1)}, bf16[2048,256]{1,0:T(8,128)(2,1)S(1)}, u32[]{:S(2)}, u32[]{:S(2)}) collective-permute-start(bf16[2048,256]{1,0:T(8,128)(2,1)S(1)} %collective-permute-done.9.fara_ref), channel_id=1, source_target_pairs={{2,3},{3,2},{6,7},{7,6}} | collective-permute-start | bytes 3145736 | tf_op jit(solution)/shard_map/ppermute | solution.py:221
  111.7 0.9 add_reduce_fusion
  112.6 0.1 pad_add_fusion.s_ref
  112.7 8.0 %shard_map.61 = (bf16[32,10,128,256]{3,2,1,0:T(8,128)(2,1)}, f32[10,32,128]{2,1,0:T(8,128)S(1)}) custom-call(s32[66]{0:T(128)S(1)} %pad_add_fusion.s_ref, bf16[32,10,128,256]{3,2,1,0:T(8,128)(2,1)} %bitcast.5, bf16[32,128,256]{2,1,0:T(8,128)(2,1)} %k_ref.15, bf16[32,128,256]{2,1,0:T(8,128)(2,1)} %v_ref.15, bf16[8224,256]{1,0:T(8,128)(2,1)} %collective-permute-done.near_ref, ...), custom_call_target="tpu_custom_call" | custom-call | flops 2684354560 | bytes 5242880 | tf_op jit(solution)/shard_map/pallas_call | solution.py:194
  120.7 0.0 collective-permute-done.12.farb_ref
  120.7 12.5 %shard_map.62 = (bf16[32,10,128,256]{3,2,1,0:T(8,128)(2,1)}, f32[10,32,128]{2,1,0:T(8,128)S(1)}) custom-call(s32[66]{0:T(128)S(1)} %pad_add_fusion.s_ref, bf16[32,10,128,256]{3,2,1,0:T(8,128)(2,1)} %bitcast.6, bf16[32,128,256]{2,1,0:T(8,128)(2,1)} %k_ref.15, bf16[32,128,256]{2,1,0:T(8,128)(2,1)} %v_ref.15, ...), custom_call_target="tpu_custom_call", output_to_operand_aliasing={{0}: (7, {})} | custom-call | flops 5368709120 | bytes 10485760 | tf_op jit(solution)/shard_map/pallas_call | solution.py:194
  133.2 0.0 collective-permute-done.10.farb_ref
  133.3 11.3 %shard_map.63 = (bf16[32,10,128,256]{3,2,1,0:T(8,128)(2,1)}, f32[10,32,128]{2,1,0:T(8,128)S(1)}) custom-call(s32[66]{0:T(128)S(1)} %pad_add_fusion.s_ref, bf16[32,10,128,256]{3,2,1,0:T(8,128)(2,1)} %bitcast.7, bf16[32,128,256]{2,1,0:T(8,128)(2,1)} %k_ref.15, bf16[32,128,256]{2,1,0:T(8,128)(2,1)} %v_ref.15, ...), custom_call_target="tpu_custom_call", output_to_operand_aliasing={{0}: (7, {})} | custom-call | flops 5368709120 | bytes 10485760 | tf_op jit(solution)/shard_map/pallas_call | solution.py:194
  144.5 0.0 collective-permute-done.8.farb_ref
  144.5 10.8 %shard_map.64 = (bf16[32,10,128,256]{3,2,1,0:T(8,128)(2,1)}, f32[10,32,128]{2,1,0:T(8,128)S(1)}) custom-call(s32[66]{0:T(128)S(1)} %pad_add_fusion.s_ref, bf16[32,10,128,256]{3,2,1,0:T(8,128)(2,1)} %bitcast.8, bf16[32,128,256]{2,1,0:T(8,128)(2,1)} %k_ref.15, bf16[32,128,256]{2,1,0:T(8,128)(2,1)} %v_ref.15, ...), custom_call_target="tpu_custom_call", output_to_operand_aliasing={{0}: (7, {})} | custom-call | flops 4697620480 | bytes 9175040 | tf_op jit(solution)/shard_map/pallas_call | solution.py:194
  155.3 0.0 collective-permute-done.6.farb_ref
  155.3 0.0 copy-start.1
  155.3 5.4 %shard_map.65 = (bf16[32,10,128,256]{3,2,1,0:T(8,128)(2,1)}, f32[10,32,128]{2,1,0:T(8,128)S(1)}) custom-call(s32[66]{0:T(128)S(1)} %pad_add_fusion.s_ref, bf16[32,10,128,256]{3,2,1,0:T(8,128)(2,1)} %bitcast.9, bf16[32,128,256]{2,1,0:T(8,128)(2,1)} %k_ref.15, bf16[32,128,256]{2,1,0:T(8,128)(2,1)} %v_ref.15, ...), custom_call_target="tpu_custom_call", output_to_operand_aliasing={{0}: (7, {})} | custom-call | flops 2013265920 | bytes 3932160 | tf_op jit(solution)/shard_map/pallas_call | solution.py:194
  160.7 0.0 collective-permute-done.4.farb_ref
  160.7 0.0 copy-done.1
  160.7 4.9 %shard_map.66 = (bf16[32,10,128,256]{3,2,1,0:T(8,128)(2,1)}, f32[10,32,128]{2,1,0:T(8,128)}) custom-call(s32[66]{0:T(128)S(1)} %pad_add_fusion.s_ref, bf16[32,10,128,256]{3,2,1,0:T(8,128)(2,1)} %bitcast.10, bf16[32,128,256]{2,1,0:T(8,128)(2,1)} %k_ref.15, bf16[32,128,256]{2,1,0:T(8,128)(2,1)} %v_ref.15, ...), custom_call_target="tpu_custom_call", output_to_operand_aliasing={{0}: (7, {})} | custom-call | flops 1342177280 | bytes 2621440 | tf_op jit(solution)/shard_map/pallas_call | solution.py:194
  (1 shorter events, 0.0 us)
Async XLA Ops:
  6.7 103.1 %collective-permute-start = (bf16[8224,256]{1,0:T(8,128)(2,1)}, bf16[8224,256]{1,0:T(8,128)(2,1)}, u32[]{:S(2)}, u32[]{:S(2)}) collective-permute-start(bf16[8224,256]{1,0:T(8,128)(2,1)} %get-tuple-element.20), channel_id=1, source_target_pairs={{0,1},{2,3},{4,5},{6,7}} | collective-permute-start | bytes 12632072 | tf_op jit(solution)/shard_map/ppermute | solution.py:221
  8.0 58.8 %collective-permute-start.11 = (bf16[2048,256]{1,0:T(8,128)(2,1)}, bf16[2048,256]{1,0:T(8,128)(2,1)S(1)}, u32[]{:S(2)}, u32[]{:S(2)}) collective-permute-start(bf16[2048,256]{1,0:T(8,128)(2,1)} %get-tuple-element.25), channel_id=1, source_target_pairs={{0,2},{1,3},{4,6},{5,7}} | collective-permute-start | bytes 3145736 | tf_op jit(solution)/shard_map/ppermute | solution.py:221
  9.3 38.5 %collective-permute-start.5 = (bf16[768,256]{1,0:T(8,128)(2,1)}, bf16[768,256]{1,0:T(8,128)(2,1)S(1)}, u32[]{:S(2)}, u32[]{:S(2)}) collective-permute-start(bf16[768,256]{1,0:T(8,128)(2,1)} %get-tuple-element.22), channel_id=1, source_target_pairs={{0,2},{1,3},{4,6},{5,7}} | collective-permute-start | bytes 1179656 | tf_op jit(solution)/shard_map/ppermute | solution.py:221
  10.6 35.2 %collective-permute-start.3 = (bf16[512,256]{1,0:T(8,128)(2,1)}, bf16[512,256]{1,0:T(8,128)(2,1)S(1)}, u32[]{:S(2)}, u32[]{:S(2)}) collective-permute-start(bf16[512,256]{1,0:T(8,128)(2,1)} %get-tuple-element.21), channel_id=1, source_target_pairs={{0,2},{1,3},{4,6},{5,7}} | collective-permute-start | bytes 786440 | tf_op jit(solution)/shard_map/ppermute | solution.py:221
  14.5 43.0 %collective-permute-start.1 = (bf16[1056,256]{1,0:T(8,128)(2,1)}, bf16[1056,256]{1,0:T(8,128)(2,1)}, u32[]{:S(2)}, u32[]{:S(2)}) collective-permute-start(bf16[1056,256]{1,0:T(8,128)(2,1)} %shard_map.60), channel_id=1, source_target_pairs={{0,2},{1,3},{4,6},{5,7}} | collective-permute-start | bytes 1622024 | tf_op jit(solution)/shard_map/ppermute | solution.py:221
  45.8 0.7 copy-start
  46.4 59.0 %collective-permute-start.9 = (bf16[2048,256]{1,0:T(8,128)(2,1)}, bf16[2048,256]{1,0:T(8,128)(2,1)S(1)}, u32[]{:S(2)}, u32[]{:S(2)}) collective-permute-start(bf16[2048,256]{1,0:T(8,128)(2,1)} %get-tuple-element.24), channel_id=1, source_target_pairs={{0,2},{1,3},{4,6},{5,7}} | collective-permute-start | bytes 3145736 | tf_op jit(solution)/shard_map/ppermute | solution.py:221
  47.7 51.8 %collective-permute-start.7 = (bf16[1792,256]{1,0:T(8,128)(2,1)}, bf16[1792,256]{1,0:T(8,128)(2,1)}, u32[]{:S(2)}, u32[]{:S(2)}) collective-permute-start(bf16[1792,256]{1,0:T(8,128)(2,1)} %get-tuple-element.23), channel_id=1, source_target_pairs={{0,2},{1,3},{4,6},{5,7}} | collective-permute-start | bytes 2752520 | tf_op jit(solution)/shard_map/ppermute | solution.py:221
  57.4 49.9 %collective-permute-start.2 = (bf16[1056,256]{1,0:T(8,128)(2,1)}, bf16[1056,256]{1,0:T(8,128)(2,1)}, u32[]{:S(2)}, u32[]{:S(2)}) collective-permute-start(bf16[1056,256]{1,0:T(8,128)(2,1)} %collective-permute-done.1.fara_ref), channel_id=1, source_target_pairs={{2,3},{3,2},{6,7},{7,6}} | collective-permute-start | bytes 1622024 | tf_op jit(solution)/shard_map/ppermute | solution.py:221
  66.8 53.9 %collective-permute-start.12 = (bf16[2048,256]{1,0:T(8,128)(2,1)S(1)}, bf16[2048,256]{1,0:T(8,128)(2,1)S(1)}, u32[]{:S(2)}, u32[]{:S(2)}) collective-permute-start(bf16[2048,256]{1,0:T(8,128)(2,1)S(1)} %collective-permute-done.11.fara_ref), channel_id=1, source_target_pairs={{2,3},{3,2},{6,7},{7,6}} | collective-permute-start | bytes 3145736 | tf_op jit(solution)/shard_map/ppermute | solution.py:221
  99.6 61.1 %collective-permute-start.4 = (bf16[512,256]{1,0:T(8,128)(2,1)}, bf16[512,256]{1,0:T(8,128)(2,1)S(1)}, u32[]{:S(2)}, u32[]{:S(2)}) collective-permute-start(bf16[512,256]{1,0:T(8,128)(2,1)} %copy-done), channel_id=1, source_target_pairs={{2,3},{3,2},{6,7},{7,6}} | collective-permute-start | bytes 786440 | tf_op jit(solution)/shard_map/ppermute | solution.py:221
  105.4 49.9 %collective-permute-start.6 = (bf16[768,256]{1,0:T(8,128)(2,1)S(1)}, bf16[768,256]{1,0:T(8,128)(2,1)S(1)}, u32[]{:S(2)}, u32[]{:S(2)}) collective-permute-start(bf16[768,256]{1,0:T(8,128)(2,1)S(1)} %collective-permute-done.5.fara_ref), channel_id=1, source_target_pairs={{2,3},{3,2},{6,7},{7,6}} | collective-permute-start | bytes 1179656 | tf_op jit(solution)/shard_map/ppermute | solution.py:221
  107.4 37.2 %collective-permute-start.8 = (bf16[1792,256]{1,0:T(8,128)(2,1)}, bf16[1792,256]{1,0:T(8,128)(2,1)S(1)}, u32[]{:S(2)}, u32[]{:S(2)}) collective-permute-start(bf16[1792,256]{1,0:T(8,128)(2,1)} %collective-permute-done.7.fara_ref), channel_id=1, source_target_pairs={{2,3},{3,2},{6,7},{7,6}} | collective-permute-start | bytes 2752520 | tf_op jit(solution)/shard_map/ppermute | solution.py:221
  109.8 23.5 %collective-permute-start.10 = (bf16[2048,256]{1,0:T(8,128)(2,1)S(1)}, bf16[2048,256]{1,0:T(8,128)(2,1)S(1)}, u32[]{:S(2)}, u32[]{:S(2)}) collective-permute-start(bf16[2048,256]{1,0:T(8,128)(2,1)S(1)} %collective-permute-done.9.fara_ref), channel_id=1, source_target_pairs={{2,3},{3,2},{6,7},{7,6}} | collective-permute-start | bytes 3145736 | tf_op jit(solution)/shard_map/ppermute | solution.py:221
  155.3 5.4 %copy-start.1 = (bf16[512,256]{1,0:T(8,128)(2,1)S(1)}, bf16[512,256]{1,0:T(8,128)(2,1)}, u32[]{:S(2)}) copy-start(bf16[512,256]{1,0:T(8,128)(2,1)} %copy-done) | copy-start | bytes 786436
